TPU v7x, 32 devices: a whole 2x2x4 slice. The times are simulated.
32 devices in a mesh: gx: 4 (over z), gy: 2 (over y), gz: 4 (over x, core).
Axes of the slice: x: 2, y: 2, z: 4, core: 2. Of those that a mesh axis runs over, the one named last changes fastest.
Arguments:
- positions: float32 [3, 8, 4, 32, 128], P(None, 'gx', 'gy', 'gz'), may hold values from 0 to 1
- shield: float32 [8, 4, 32, 128], P('gx', 'gy', 'gz'), may hold values from 0.3 to 1
- width: float32 [8, 4, 32, 128], P('gx', 'gy', 'gz'), may hold values from 0.5 to 2
- hardness: float32 [8, 4, 32, 128], P('gx', 'gy', 'gz'), may hold values from 0.5 to 2
- softness: float32 [8, 4, 32, 128], P('gx', 'gy', 'gz'), may hold values from 0.5 to 2
- coupling: float32 [8, 4, 32, 128], P('gx', 'gy', 'gz'), may hold values from -0.45 to 0.45
- pair_bits: int32 [8, 4, 32], P('gx', 'gy', 'gz'), may hold values from 8192 to 134217727
- right_side: float32 [4, 8, 4, 32, 128], P(None, 'gx', 'gy', 'gz'), may hold values from -7 to 7
Outputs:
- solution: float32 [4, 8, 4, 32, 128], P(None, 'gx', 'gy', 'gz')
- residual: float32 [4, 8, 4, 32, 128], P(None, 'gx', 'gy', 'gz')
All inputs are finite; a program needn't handle non-finite values.
Results may differ from a plain program's by a relative error of at most 0.0018.
Values sent between devices are 32-bit elements; how exact they have to be, the bound alone decides.
No kernel may reach another device: no remote copies, remote signals or barrier semaphores. Data moves between devices by JAX's collectives and lax.ppermute only.
A program may use at most 128 MiB of HBM per device.

v0:
```python
import jax
import jax.numpy as jnp
from jax import lax
from jax.sharding import PartitionSpec as P

ITERS = 3


coulomb_scale = 0.002
response_scale = 0.003


def extended(block, sides, width):
    for axis, dim in sides:
        count = lax.axis_size(axis)
        forward = [(i, i + 1) for i in range(count - 1)]
        backward = [(target, source) for source, target in forward]
        low = lax.ppermute(
            lax.slice_in_dim(block, block.shape[dim] - width, None, axis=dim), axis, forward
        )
        high = lax.ppermute(lax.slice_in_dim(block, 0, width, axis=dim), axis, backward)
        block = jnp.concatenate([low, block, high], axis=dim)
    return block


def index_tuple(values):
    return tuple((jnp.asarray(value).astype(jnp.int32) for value in values))


def pair_terms(own_params, partner, offset_code, own_bits):
    shift_first = (offset_code // 9 - 1).astype(jnp.float32)
    shift_second = (offset_code // 3 % 3 - 1).astype(jnp.float32)
    shift_third = (offset_code % 3 - 1).astype(jnp.float32)

    def separation(column, shift):
        return shift + (partner[column][:, None, :] - own_params[column][:, :, None])

    first = separation(0, shift_first)
    second = separation(1, shift_second)
    third = separation(2, shift_third)
    distance = first * first + second * second + third * third
    coulomb = coulomb_scale * lax.rsqrt(
        distance + own_params[3][:, :, None] * partner[3][:, None, :]
    )
    response = response_scale * jnp.exp(
        -distance / (own_params[4][:, :, None] + partner[4][:, None, :])
    )
    listed = jnp.right_shift(own_bits, offset_code) & 1 > 0
    tile_size = own_params.shape[2]
    diagonal_mask = lax.broadcasted_iota(
        jnp.int32, (tile_size, tile_size), 0
    ) == lax.broadcasted_iota(jnp.int32, (tile_size, tile_size), 1)
    kept = listed[:, None, None] & jnp.logical_not(diagonal_mask[None] & (offset_code == 13))
    empty_pair = jnp.zeros_like(distance)
    return (
        jnp.where(kept, coulomb, empty_pair).astype(jnp.bfloat16),
        jnp.where(kept, response, empty_pair).astype(jnp.bfloat16),
    )


def tile_block(padded, offset_code, extent):
    fields = padded.shape[0]
    tile_size = padded.shape[4]
    start = index_tuple((0, offset_code // 9, offset_code // 3 % 3, offset_code % 3, 0))
    block = lax.dynamic_slice(padded, start, (fields, extent[0], extent[1], extent[2], tile_size))
    return block.reshape(fields, extent[0] * extent[1] * extent[2], tile_size)


def static_block(padded, offset_code, extent):
    first = offset_code // 9
    second = offset_code // 3 % 3
    third = offset_code % 3
    block = padded[
        :, first : first + extent[0], second : second + extent[1], third : third + extent[2]
    ]
    return block.reshape(padded.shape[0], extent[0] * extent[1] * extent[2], padded.shape[4])


def spread_ghosts(vector, extent):
    shaped = vector.reshape(4, extent[0], extent[1], extent[2], vector.shape[2])
    return extended(shaped, (("gx", 1), ("gy", 2), ("gz", 3)), 1)


def split_parts(padded):
    upper = padded.astype(jnp.bfloat16)
    lower = (padded - upper.astype(jnp.float32)).astype(jnp.bfloat16)
    return jnp.concatenate([upper[:2], lower[:2], upper[2:], lower[2:]], axis=0)


def inner_local(vector, other_vector):
    return jnp.sum((vector * other_vector).reshape(2, 2, -1), axis=(0, 2))


def two_products(vector, applied):
    return lax.psum((inner_local(vector, vector), inner_local(vector, applied)), ("gx", "gy", "gz"))


def widen(scalars):
    return jnp.concatenate([scalars, scalars]).reshape(4, 1, 1)


def on_device(positions, shield, width, hardness, softness, coupling, pair_bits, right_side):
    tiles_x, tiles_y, tiles_z, tile_size = hardness.shape
    extent = (tiles_x, tiles_y, tiles_z)
    tile_count = tiles_x * tiles_y * tiles_z
    params = jnp.concatenate([positions, shield[None], width[None]], axis=0)
    joined = extended(
        jnp.concatenate([params, right_side], axis=0), (("gx", 1), ("gy", 2), ("gz", 3)), 1
    )
    params_pad = joined[:5]
    first_pad = joined[5:]
    own_params = params_pad[:, 1:-1, 1:-1, 1:-1].reshape(5, tile_count, tile_size)
    own_bits = pair_bits.reshape(tile_count)

    def build(offset_code, carry):
        store_coulomb, store_response, row_coulomb, row_response = carry
        offset_code = offset_code.astype(jnp.int32)
        partner = tile_block(params_pad, offset_code, extent)
        coulomb, response = pair_terms(own_params, partner, offset_code, own_bits)
        store_coulomb = lax.dynamic_update_index_in_dim(store_coulomb, coulomb, offset_code, 0)
        store_response = lax.dynamic_update_index_in_dim(store_response, response, offset_code, 0)
        row_coulomb = row_coulomb + jnp.sum(coulomb.astype(jnp.float32), axis=2)
        row_response = row_response + jnp.sum(response.astype(jnp.float32), axis=2)
        return (store_coulomb, store_response, row_coulomb, row_response)

    store_zeros = jnp.zeros((27, tile_count, tile_size, tile_size), jnp.bfloat16)
    flat_zeros = jnp.zeros((tile_count, tile_size), jnp.float32)
    store_coulomb, store_response, row_coulomb, row_response = lax.fori_loop(
        0, 27, build, (store_zeros, store_zeros, flat_zeros, flat_zeros)
    )
    diagonal_charge = hardness.reshape(tile_count, tile_size) + row_coulomb
    diagonal_potential = softness.reshape(tile_count, tile_size) + row_response
    linking = coupling.reshape(tile_count, tile_size)

    def operate(padded, vector):
        parts_pad = split_parts(padded)
        stacked = jnp.stack(
            [static_block(parts_pad, offset_code, extent) for offset_code in range(27)], axis=0
        )
        charge_terms = jnp.einsum(
            "otij,oftj->fti", store_coulomb, stacked[:, :4], preferred_element_type=jnp.float32
        )
        potential_terms = jnp.einsum(
            "otij,oftj->fti", store_response, stacked[:, 4:], preferred_element_type=jnp.float32
        )
        pair_charge = charge_terms[:2] + charge_terms[2:]
        pair_potential = potential_terms[:2] + potential_terms[2:]
        image_charge = diagonal_charge * vector[:2] + pair_charge + linking * vector[2:]
        image_potential = diagonal_potential * vector[2:] - pair_potential + linking * vector[:2]
        return jnp.concatenate([image_charge, image_potential], axis=0)

    rhs_flat = right_side.reshape(4, tile_count, tile_size)
    solution = jnp.zeros_like(rhs_flat)
    applied = operate(first_pad, rhs_flat)
    norm_now, product = two_products(rhs_flat, applied)
    step_size = norm_now / product
    remainder = rhs_flat
    direction = rhs_flat
    along = applied
    for iteration in range(ITERS):
        solution = solution + widen(step_size) * direction
        remainder = remainder - widen(step_size) * along
        if iteration + 1 < ITERS:
            applied = operate(spread_ghosts(remainder, extent), remainder)
            norm_next, product = two_products(remainder, applied)
            beta_ratio = norm_next / norm_now
            step_size = norm_next / (product - beta_ratio * norm_next / step_size)
            direction = remainder + widen(beta_ratio) * direction
            along = applied + widen(beta_ratio) * along
            norm_now = norm_next
    final_image = operate(spread_ghosts(solution, extent), solution)
    residual = rhs_flat - final_image
    shape_out = (4, tiles_x, tiles_y, tiles_z, tile_size)
    return (solution.reshape(shape_out), residual.reshape(shape_out))


def solution(mesh):
    return jax.shard_map(
        on_device,
        mesh=mesh,
        in_specs=(
            P(None, "gx", "gy", "gz", None),
            P("gx", "gy", "gz", None),
            P("gx", "gy", "gz", None),
            P("gx", "gy", "gz", None),
            P("gx", "gy", "gz", None),
            P("gx", "gy", "gz", None),
            P("gx", "gy", "gz"),
            P(None, "gx", "gy", "gz", None),
        ),
        out_specs=(P(None, "gx", "gy", "gz", None), P(None, "gx", "gy", "gz", None)),
        check_vma=False,
    )
```

profile of v0, /device:TPU:0, one launch (start us, length us, event | category | flops | bytes accessed | tf_op | source)
XLA Modules:
  0.0 624.8 jit_solution(3941174055811860574)
XLA Ops:
  2.9 5.6 collective-permute-start
  27.8 282.4 %while.23 = (s32[]{:T(128)}, bf16[27,32,128,128]{3,2,0,1:T(8,128)(2,1)}, bf16[27,32,128,128]{3,2,0,1:T(8,128)(2,1)}, f32[32,128]{1,0:T(8,128)S(1)}, f32[32,128]{...) while((s32[]{:T(128)}, ...), condition=%wide.region_6.7_spmd.clone, body=%wide.region_3.6_spmd.clone.sunk | while | flops 26271884 | bytes 2933673 | solution.py:128
  27.9 5.2 fusion.83
  33.2 5.0 convert_reduce_fusion.3
  38.4 5.2 fusion.83
  43.6 5.0 convert_reduce_fusion.3
  48.9 5.2 fusion.83
  54.1 5.0 convert_reduce_fusion.3
  59.4 5.2 fusion.83
  64.6 5.0 convert_reduce_fusion.3
  69.9 5.2 fusion.83
  75.1 5.0 convert_reduce_fusion.3
  80.3 5.3 fusion.83
  85.6 5.0 convert_reduce_fusion.3
  90.8 5.2 fusion.83
  96.0 5.0 convert_reduce_fusion.3
  101.3 5.2 fusion.83
  106.5 5.0 convert_reduce_fusion.3
  111.7 5.2 fusion.83
  116.9 5.0 convert_reduce_fusion.3
  122.2 5.2 fusion.83
  127.4 5.0 convert_reduce_fusion.3
  132.6 5.2 fusion.83
  137.8 5.0 convert_reduce_fusion.3
  143.1 5.2 fusion.83
  148.3 5.0 convert_reduce_fusion.3
  153.5 5.2 fusion.83
  158.7 5.0 convert_reduce_fusion.3
  164.0 5.2 fusion.83
  169.2 5.0 convert_reduce_fusion.3
  174.4 5.2 fusion.83
  179.6 5.0 convert_reduce_fusion.3
  184.8 5.2 fusion.83
  190.1 5.0 convert_reduce_fusion.3
  195.3 5.2 fusion.83
  200.5 5.0 convert_reduce_fusion.3
  205.8 5.2 fusion.83
  211.0 5.0 convert_reduce_fusion.3
  216.2 5.2 fusion.83
  221.4 5.0 convert_reduce_fusion.3
  226.7 5.2 fusion.83
  231.9 5.0 convert_reduce_fusion.3
  237.1 5.3 fusion.83
  242.4 5.0 convert_reduce_fusion.3
  247.6 5.3 fusion.83
  252.9 5.0 convert_reduce_fusion.3
  258.1 5.2 fusion.83
  263.4 5.0 convert_reduce_fusion.3
  268.6 5.2 fusion.83
  279.1 5.2 fusion.83
  289.5 5.2 fusion.83
  299.9 5.2 fusion.83
  305.1 5.0 convert_reduce_fusion.3
  312.6 13.1 %convolution_bitcast_fusion.6 = f32[4,32,128]{2,0,1:T(4,128)S(1)} fusion(bf16[27,32,128,128]{3,2,0,1:T(8,128)(2,1)} %get-tuple-element.243, bf16[27,8,32,128]{3,1,0,2:T(8,128)(2,1)S(1)} %constant_dynamic-update-slice_fusion), kind=kOutput, calls=%fused_computation.39 | convolution fusion | flops 113246208 | bytes 29261824 | tf_op jit(solution)/shard_map/otij,oftj->fti/dot_general | solution.py:143
  325.7 13.4 %convolution_bitcast_fusion.7 = f32[4,32,128]{2,0,1:T(4,128)S(1)} fusion(bf16[27,32,128,128]{3,2,0,1:T(8,128)(2,1)} %get-tuple-element.241, bf16[27,8,32,128]{3,1,0,2:T(8,128)(2,1)S(1)} %constant_dynamic-update-slice_fusion), kind=kOutput, calls=%fused_computation.40 | convolution fusion | flops 113246208 | bytes 29261824 | tf_op jit(solution)/shard_map/otij,oftj->fti/dot_general | solution.py:140
  339.6 45.1 %all-reduce.2 = (f32[2]{0:T(128)S(1)}, f32[2]{0:T(128)S(1)}) all-reduce(f32[2]{0:T(128)S(1)} %reduce_sum.132, f32[2]{0:T(128)S(1)} %reduce_sum.135), channel_id=1, replica_groups=mesh['gx'=4,'gy'=2,'gz'=4] {'gx','gy','gz'}, use_global_device_ids=true, to_apply=%region_2.3 | all-reduce | flops 4 | bytes 32 | tf_op jit(solution)/shard_map/psum | solution.py:95
  407.9 13.1 %convolution_bitcast_fusion.4 = f32[4,32,128]{2,0,1:T(4,128)S(1)} fusion(bf16[27,32,128,128]{3,2,0,1:T(8,128)(2,1)} %get-tuple-element.243, bf16[27,8,32,128]{3,1,0,2:T(8,128)(2,1)S(1)} %constant_dynamic-update-slice_fusion.29), kind=kOutput, calls=%fused_computation.37 | convolution fusion | flops 113246208 | bytes 29261824 | tf_op jit(solution)/shard_map/otij,oftj->fti/dot_general | solution.py:143
  420.9 13.4 %convolution_bitcast_fusion.5 = f32[4,32,128]{2,0,1:T(4,128)S(1)} fusion(bf16[27,32,128,128]{3,2,0,1:T(8,128)(2,1)} %get-tuple-element.241, bf16[27,8,32,128]{3,1,0,2:T(8,128)(2,1)S(1)} %constant_dynamic-update-slice_fusion.29), kind=kOutput, calls=%fused_computation.38 | convolution fusion | flops 113246208 | bytes 29261824 | tf_op jit(solution)/shard_map/otij,oftj->fti/dot_general | solution.py:140
  434.7 44.7 %all-reduce.1 = (f32[2]{0:T(128)S(1)}, f32[2]{0:T(128)S(1)}) all-reduce(f32[2]{0:T(128)S(1)} %reduce_sum.138, f32[2]{0:T(128)S(1)} %reduce_sum.141), channel_id=1, replica_groups=mesh['gx'=4,'gy'=2,'gz'=4] {'gx','gy','gz'}, use_global_device_ids=true, to_apply=%region_12.13 | all-reduce | flops 4 | bytes 32 | tf_op jit(solution)/shard_map/psum | solution.py:95
  502.8 13.4 %convolution_bitcast_fusion.3 = f32[4,32,128]{2,0,1:T(4,128)S(1)} fusion(bf16[27,32,128,128]{3,2,0,1:T(8,128)(2,1)} %get-tuple-element.241, bf16[27,8,32,128]{3,1,0,2:T(8,128)(2,1)S(1)} %constant_dynamic-update-slice_fusion.58), kind=kOutput, calls=%fused_computation.36 | convolution fusion | flops 113246208 | bytes 29261824 | tf_op jit(solution)/shard_map/otij,oftj->fti/dot_general | solution.py:140
  516.1 13.1 %convolution_bitcast_fusion.2 = f32[4,32,128]{2,0,1:T(4,128)S(1)} fusion(bf16[27,32,128,128]{3,2,0,1:T(8,128)(2,1)} %get-tuple-element.243, bf16[27,8,32,128]{3,1,0,2:T(8,128)(2,1)S(1)} %constant_dynamic-update-slice_fusion.58), kind=kOutput, calls=%fused_computation.35 | convolution fusion | flops 113246208 | bytes 29261824 | tf_op jit(solution)/shard_map/otij,oftj->fti/dot_general | solution.py:143
  529.6 44.8 %all-reduce = (f32[2]{0:T(128)S(1)}, f32[2]{0:T(128)S(1)}) all-reduce(f32[2]{0:T(128)S(1)} %reduce_sum.144, f32[2]{0:T(128)S(1)} %reduce_sum.147), channel_id=1, replica_groups=mesh['gx'=4,'gy'=2,'gz'=4] {'gx','gy','gz'}, use_global_device_ids=true, to_apply=%region_18.19 | all-reduce | flops 4 | bytes 32 | tf_op jit(solution)/shard_map/psum | solution.py:95
  597.5 13.4 %convolution_bitcast_fusion.1 = f32[4,32,128]{2,0,1:T(4,128)S(1)} fusion(bf16[27,32,128,128]{3,2,0,1:T(8,128)(2,1)} %get-tuple-element.241, bf16[27,8,32,128]{3,1,0,2:T(8,128)(2,1)S(1)} %constant_dynamic-update-slice_fusion.85), kind=kOutput, calls=%fused_computation.34 | convolution fusion | flops 113246208 | bytes 29261824 | tf_op jit(solution)/shard_map/otij,oftj->fti/dot_general | solution.py:140
  610.9 13.1 %convolution_bitcast_fusion = f32[4,32,128]{2,0,1:T(4,128)S(1)} fusion(bf16[27,32,128,128]{3,2,0,1:T(8,128)(2,1)} %get-tuple-element.243, bf16[27,8,32,128]{3,1,0,2:T(8,128)(2,1)S(1)} %constant_dynamic-update-slice_fusion.85), kind=kOutput, calls=%fused_computation.33 | convolution fusion | flops 113246208 | bytes 29261824 | tf_op jit(solution)/shard_map/otij,oftj->fti/dot_general | solution.py:143
  (522 shorter events, 110.8 us)
Async XLA Ops:
  0.6 16.6 %copy-start = (f32[4,2,2,8,128]{4,3,2,1,0:T(8,128)S(1)}, f32[4,2,2,8,128]{4,3,2,1,0:T(8,128)}, u32[]{:S(2)}) copy-start(f32[4,2,2,8,128]{4,3,2,1,0:T(8,128)} %param.17) | copy-start | bytes 196612
  0.6 19.3 %copy-start.4 = (f32[2,2,8,128]{3,2,1,0:T(8,128)S(1)}, f32[2,2,8,128]{3,2,1,0:T(8,128)}, u32[]{:S(2)}) copy-start(f32[2,2,8,128]{3,2,1,0:T(8,128)} %param.12) | copy-start | bytes 49156
  0.7 19.3 %copy-start.5 = (f32[2,2,8,128]{3,2,1,0:T(8,128)S(1)}, f32[2,2,8,128]{3,2,1,0:T(8,128)}, u32[]{:S(2)}) copy-start(f32[2,2,8,128]{3,2,1,0:T(8,128)} %param.11) | copy-start | bytes 49156
  0.7 19.3 %copy-start.3 = (f32[3,2,2,8,128]{4,3,2,1,0:T(8,128)S(1)}, f32[3,2,2,8,128]{4,3,2,1,0:T(8,128)}, u32[]{:S(2)}) copy-start(f32[3,2,2,8,128]{4,3,2,1,0:T(8,128)} %param.10) | copy-start | bytes 147460
  1.6 7.7 %collective-permute-start.1 = (f32[9,1,2,8,128]{4,3,2,1,0:T(8,128)S(1)}, f32[9,1,2,8,128]{4,3,2,1,0:T(8,128)S(1)}, u32[]{:S(2)}, u32[]{:S(2)}) collective-permute-start(f32[9,1,2,8,128]{4,3,2,1,0:T(8,128)S(1)} %get-tuple-element.453), channel_id=1, source_target_pairs={{8,0},{16,8},{24,16},{9,1},{17,9},{25,17},{10,2},{18,10},{26,18},{... | collective-permute-start | bytes 221192 | tf_op jit(solution)/shard_map/ppermute | solution.py:21
  2.9 7.6 %collective-permute-start = (f32[9,1,2,8,128]{4,3,2,1,0:T(8,128)S(1)}, f32[9,1,2,8,128]{4,3,2,1,0:T(8,128)S(1)}, u32[]{:S(2)}, u32[]{:S(2)}) collective-permute-start(f32[9,1,2,8,128]{4,3,2,1,0:T(8,128)S(1)} %get-tuple-element.452), channel_id=1, source_target_pairs={{0,8},{8,16},{16,24},{1,9},{9,17},{17,25},{2,10},{10,18},{18,26},{... | collective-permute-start | bytes 221192 | tf_op jit(solution)/shard_map/ppermute | solution.py:18
  11.4 7.0 %collective-permute-start.3 = (f32[9,4,1,8,128]{4,3,2,1,0:T(8,128)S(1)}, f32[9,4,1,8,128]{4,3,2,1,0:T(8,128)S(1)}, u32[]{:S(2)}, u32[]{:S(2)}) collective-permute-start(f32[9,4,1,8,128]{4,3,2,1,0:T(8,128)S(1)} %get-tuple-element.429), channel_id=1, source_target_pairs={{4,0},{5,1},{6,2},{7,3},{12,8},{13,9},{14,10},{15,11},{20,16},{21,... | collective-permute-start | bytes 442376 | tf_op jit(solution)/shard_map/ppermute | solution.py:21
  12.7 7.2 %collective-permute-start.2 = (f32[9,4,1,8,128]{4,3,2,1,0:T(8,128)S(1)}, f32[9,4,1,8,128]{4,3,2,1,0:T(8,128)S(1)}, u32[]{:S(2)}, u32[]{:S(2)}) collective-permute-start(f32[9,4,1,8,128]{4,3,2,1,0:T(8,128)S(1)} %get-tuple-element.428), channel_id=1, source_target_pairs={{0,4},{1,5},{2,6},{3,7},{8,12},{9,13},{10,14},{11,15},{16,20},{17,... | collective-permute-start | bytes 442376 | tf_op jit(solution)/shard_map/ppermute | solution.py:18
  20.1 4.4 collective-permute-start.5
  21.4 3.9 collective-permute-start.4
  25.5 1.0 copy-start.1
  26.7 1.1 slice-start
  325.7 13.4 %copy-start.8 = (f32[2,2,8,128]{3,2,1,0:T(8,128)S(1)}, f32[2,2,8,128]{3,2,1,0:T(8,128)}, u32[]{:S(2)}) copy-start(f32[2,2,8,128]{3,2,1,0:T(8,128)} %param.14) | copy-start | bytes 49156
  325.7 13.4 %copy-start.9 = (f32[2,2,8,128]{3,2,1,0:T(8,128)S(1)}, f32[2,2,8,128]{3,2,1,0:T(8,128)}, u32[]{:S(2)}) copy-start(f32[2,2,8,128]{3,2,1,0:T(8,128)} %param.13) | copy-start | bytes 49156
  325.7 13.4 %copy-start.6 = (f32[2,2,8,128]{3,2,1,0:T(8,128)S(1)}, f32[2,2,8,128]{3,2,1,0:T(8,128)}, u32[]{:S(2)}) copy-start(f32[2,2,8,128]{3,2,1,0:T(8,128)} %param.15) | copy-start | bytes 49156
  325.7 13.4 %copy-start.7 = (f32[2,2,2,8,128]{4,0,3,2,1:T(2,128)S(1)}, f32[2,2,2,8,128]{4,0,3,2,1:T(2,128)}, u32[]{:S(2)}) copy-start(f32[2,2,2,8,128]{4,0,3,2,1:T(2,128)} %copy.141) | copy-start | bytes 98308
  385.0 5.9 collective-permute-start.7
  386.3 6.1 collective-permute-start.6
  392.4 6.2 collective-permute-start.9
  393.7 6.4 %collective-permute-start.8 = (f32[4,4,1,8,128]{4,3,2,1,0:T(8,128)S(1)}, f32[4,4,1,8,128]{4,3,2,1,0:T(8,128)S(1)}, u32[]{:S(2)}, u32[]{:S(2)}) collective-permute-start(f32[4,4,1,8,128]{4,3,2,1,0:T(8,128)S(1)} %get-tuple-element.458), channel_id=1, source_target_pairs={{0,4},{1,5},{2,6},{3,7},{8,12},{9,13},{10,14},{11,15},{16,20},{17,... | collective-permute-start | bytes 196616 | tf_op jit(solution)/shard_map/ppermute | solution.py:18
  400.2 4.7 collective-permute-start.11
  401.5 3.9 collective-permute-start.10
  479.9 5.9 collective-permute-start.13
  481.2 6.1 collective-permute-start.12
  487.3 6.2 collective-permute-start.15
  488.6 6.4 %collective-permute-start.14 = (f32[4,4,1,8,128]{4,3,2,1,0:T(8,128)S(1)}, f32[4,4,1,8,128]{4,3,2,1,0:T(8,128)S(1)}, u32[]{:S(2)}, u32[]{:S(2)}) collective-permute-start(f32[4,4,1,8,128]{4,3,2,1,0:T(8,128)S(1)} %get-tuple-element.456), channel_id=1, source_target_pairs={{0,4},{1,5},{2,6},{3,7},{8,12},{9,13},{10,14},{11,15},{16,20},{17,... | collective-permute-start | bytes 196616 | tf_op jit(solution)/shard_map/ppermute | solution.py:18
  495.1 4.4 collective-permute-start.17
  496.4 3.9 collective-permute-start.16
  574.6 20.9 %copy-start.2 = (f32[4,2,2,8,128]{4,3,2,1,0:T(8,128)}, f32[4,2,2,8,128]{4,3,2,1,0:T(8,128)S(1)}, u32[]{:S(2)}) copy-start(f32[4,2,2,8,128]{4,3,2,1,0:T(8,128)S(1)} %multiply_add_fusion.2) | copy-start | bytes 196612
  574.7 5.9 collective-permute-start.19
  576.0 6.1 collective-permute-start.18
  582.1 6.2 collective-permute-start.21
  583.4 6.4 %collective-permute-start.20 = (f32[4,4,1,8,128]{4,3,2,1,0:T(8,128)S(1)}, f32[4,4,1,8,128]{4,3,2,1,0:T(8,128)S(1)}, u32[]{:S(2)}, u32[]{:S(2)}) collective-permute-start(f32[4,4,1,8,128]{4,3,2,1,0:T(8,128)S(1)} %get-tuple-element.454), channel_id=1, source_target_pairs={{0,4},{1,5},{2,6},{3,7},{8,12},{9,13},{10,14},{11,15},{16,20},{17,... | collective-permute-start | bytes 196616 | tf_op jit(solution)/shard_map/ppermute | solution.py:18
  589.9 4.5 collective-permute-start.23
  591.2 3.9 collective-permute-start.22
where the time goes:
time: 629 us; the launch traced here: 625 us
  other arithmetic  283 us (45%)
  blocking collectives  135 us (21%)
  matrix products  106 us (17%)
  starting transfers between devices  65.2 us (10%)
  waiting for transfers between devices  16.2 us (3%)
  local copies, waits for them, and re-layouts  12.7 us (2%)
    dynamic_update_slice x27, other arithmetic, build(): lax.dynamic_update_index_in_dim(store_response, response, offset_code, 0)  141 us
    reduce_sum x27, other arithmetic, build(): row_response = row_response + jnp.sum(response.astype(jnp.float32), axis=2)  135 us
    psum x3, blocking collectives, two_products(): lax.psum((inner_local(vector, vector), inner_local(vector, applied)), ('g...  135 us
    dot_general x4, matrix products, operate(): jnp.einsum('otij,oftj->fti', store_coulomb, stacked[:, :4], preferred_ele...  53.5 us
    dot_general x4, matrix products, operate(): jnp.einsum('otij,oftj->fti', store_response, stacked[:, 4:], preferred_el...  52.3 us
    ppermute x12, starting transfers between devices, extended(): lax.ppermute(lax.slice_in_dim(block, block.shape[dim] - width, None, axis...  49.7 us
    ppermute x12, starting transfers between devices, extended(): lax.ppermute(lax.slice_in_dim(block, 0, width, axis=dim), axis, backward)  15.5 us
    ppermute x12, waiting for transfers between devices, extended(): lax.ppermute(lax.slice_in_dim(block, block.shape[dim] - width, None, axis...  14.9 us
  transfers between devices with their start and end apart: 24, of which 16 were waited for; matrix products, arithmetic and copies ran while one was open for 0% of the time, Pallas kernels for 0%

commit v1 on v0

v1 whole, which is shorter than its diff:
```python
import math

import jax
import jax.numpy as jnp
import numpy as np
from jax import lax
from jax.experimental import pallas as pl
from jax.experimental.pallas import tpu as pltpu
from jax.sharding import PartitionSpec as P

ITERS = 3

coulomb_scale = 0.002
response_scale = 0.003
length_scale = 1.0 / coulomb_scale
width_scale = -math.log(2.0) * length_scale * length_scale

SHIFT = 3.0

AXES = ("gx", "gy", "gz")
HALO_ORDER = (("gz", 2), ("gx", 0), ("gy", 1))
PARTS = 3
SELF = 13
BUILD_SLOTS = 4
BUILD_RING = 4
APPLY_CHUNK = 8
APPLY_COPY = 2
APPLY_RING = 10


class Piece:
    def __init__(self, array, boxes):
        self.array = array
        self.boxes = boxes

    def face(self, dim, level):
        rows, boxes = [], []
        offset = 0
        for origin, shape in self.boxes:
            volume = shape[0] * shape[1] * shape[2]
            if origin[dim] <= level < origin[dim] + shape[dim]:
                part = self.array[:, offset : offset + volume]
                part = part.reshape((part.shape[0],) + shape + part.shape[2:])
                part = lax.slice_in_dim(part, level - origin[dim], level - origin[dim] + 1, axis=dim + 1)
                cut = tuple(1 if d == dim else shape[d] for d in range(3))
                rows.append(part.reshape(part.shape[0], -1, part.shape[-1]))
                boxes.append((tuple(level if d == dim else origin[d] for d in range(3)), cut))
            offset += volume
        return rows, boxes


def whole_face(pieces, dim, level):
    rows, boxes = [], []
    for piece in pieces:
        more_rows, more_boxes = piece.face(dim, level)
        rows += more_rows
        boxes += more_boxes
    return (jnp.concatenate(rows, axis=1) if len(rows) > 1 else rows[0]), boxes


def moved(boxes, dim, level):
    return [(tuple(level if d == dim else o[d] for d in range(3)), s) for o, s in boxes]


def extended(block, extent):
    pieces = [Piece(block, [((0, 0, 0), extent)])]
    for axis, dim in HALO_ORDER:
        count = lax.axis_size(axis)
        if count == 1:
            continue
        size = extent[dim]
        first, boxes = whole_face(pieces, dim, 0)
        last, _ = whole_face(pieces, dim, size - 1)
        if count == 2:
            sent = jnp.where(lax.axis_index(axis) == 0, last, first)
            got = lax.ppermute(sent, axis, [(0, 1), (1, 0)])
            pieces = pieces + [Piece(got, moved(boxes, dim, size))]
        else:
            forward = [(i, (i + 1) % count) for i in range(count)]
            backward = [(target, source) for source, target in forward]
            low = lax.ppermute(last, axis, forward)
            high = lax.ppermute(first, axis, backward)
            pieces = pieces + [
                Piece(low, moved(boxes, dim, -1)),
                Piece(high, moved(boxes, dim, size)),
            ]
    joined = jnp.concatenate([piece.array for piece in pieces], axis=1)
    return joined, [box for piece in pieces for box in piece.boxes]


def storage_rows(boxes, extent, counts):
    rows = {}
    offset = 0
    for origin, shape in boxes:
        for a in range(shape[0]):
            for b in range(shape[1]):
                for c in range(shape[2]):
                    rows[(origin[0] + a, origin[1] + b, origin[2] + c)] = offset
                    offset += 1

    def row_of(coord):
        fixed = list(coord)
        for axis, dim in HALO_ORDER:
            outside = not 0 <= fixed[dim] < extent[dim]
            if outside and counts[axis] == 1:
                fixed[dim] = 0
            elif outside and counts[axis] == 2:
                fixed[dim] = extent[dim]
        return rows[tuple(fixed)]

    return row_of


def candidate_table(boxes, extent, counts):
    row_of = storage_rows(boxes, extent, counts)
    table = []
    for x in range(extent[0]):
        for y in range(extent[1]):
            for z in range(extent[2]):
                own = (x * extent[1] + y) * extent[2] + z
                for a in range(3):
                    for b in range(3):
                        for c in range(3):
                            partner = row_of((x + a - 1, y + b - 1, z + c - 1))
                            assert own < 255 and partner < 256
                            table.append(own | a << 8 | b << 10 | c << 12 | partner << 14)
    return np.asarray(table, np.int32)


def list_kernel(bits_ref, table_ref, list_ref, count_ref):
    tiles = bits_ref.shape[0]
    pad = list_ref.shape[0] - 27 * tiles

    def visit(tile, filled):
        word = bits_ref[tile]
        list_ref[tile] = table_ref[tile * 27 + SELF]
        for code in range(27):
            if code != SELF:
                list_ref[filled] = table_ref[tile * 27 + code]
                filled = filled + ((word >> code) & 1)
        return filled

    filled = lax.fori_loop(0, tiles, visit, jnp.int32(tiles))
    for extra in range(pad):
        list_ref[filled + extra] = tiles
    count_ref[0] = filled


def split_rows(values):
    parts = []
    rest = values
    for _ in range(PARTS):
        part = rest.astype(jnp.bfloat16).astype(jnp.float32)
        parts.append(part)
        rest = rest - part
    return parts


def fill_vectors(source_ref, first_row, rows_all, vec_ref):
    def one(tile, carry):
        values = source_ref[pl.ds(first_row + tile, 4, stride=rows_all), :]
        parts = split_rows(values)
        stacked = jnp.concatenate(parts + [jnp.ones_like(values)], axis=0)
        vec_ref[tile] = stacked.astype(jnp.bfloat16)
        return carry

    lax.fori_loop(0, rows_all, one, 0, unroll=8)


def pair_parts(total):
    joined = total[0:4] + total[4:8] + total[8:12]
    return joined[0:2, 0:128], joined[2:4, 128:256]


def image_rows(values, pair_charge, pair_potential, diag_charge, diag_potential, linking):
    charge, potential = values[0:2], values[2:4]
    image_charge = diag_charge * charge + pair_charge + linking * potential
    image_potential = diag_potential * potential - pair_potential + linking * charge
    return jnp.concatenate([image_charge, image_potential], axis=0)


def block_product(vectors, block):
    return lax.dot_general(vectors, block, (((1,), (1,)), ((), ())), preferred_element_type=jnp.float32)


def build_kernel(list_ref, count_ref, joined_ref, own_ref, hard_ref, soft_ref, link_ref,
                 store_ref, diag_charge_ref, diag_potential_ref, image_ref,
                 row_ref, spread_ref, vec_ref, sum_ref, even_ref, odd_ref, sems):
    tiles = hard_ref.shape[0]
    rows_all = vec_ref.shape[0]
    size = hard_ref.shape[1]
    count = count_ref[0]

    field = lax.broadcasted_iota(jnp.int32, (8, size), 0)
    scale = jnp.where(field < 4, jnp.float32(length_scale), jnp.float32(width_scale))

    def prepare(tile, carry):
        row_ref[tile] = joined_ref[pl.ds(tile, 8, stride=rows_all), :] * scale
        return carry

    lax.fori_loop(0, rows_all, prepare, 0, unroll=8)
    fill_vectors(joined_ref, 5 * rows_all, rows_all, vec_ref)

    line = lax.broadcasted_iota(jnp.int32, (32, 5 * size), 0)
    chosen = lax.broadcasted_iota(jnp.int32, (32, 5 * size), 1) // size
    select = jnp.where(((line & 7) == chosen) & (line < 24), 1.0, 0.0).astype(jnp.bfloat16)

    def spread(tile, carry):
        params = row_ref[tile]
        stacked = jnp.concatenate(split_rows(params) + [jnp.zeros_like(params)], axis=0)
        spread_ref[tile] = lax.dot_general(
            stacked.astype(jnp.bfloat16), select, (((0,), (0,)), ((), ())), preferred_element_type=jnp.float32)
        sum_ref[tile] = jnp.zeros(sum_ref.shape[1:], jnp.float32)
        return carry

    lax.fori_loop(0, tiles, spread, 0, unroll=2)
    sum_ref[tiles] = jnp.zeros(sum_ref.shape[1:], jnp.float32)

    def multiply(ring_ref, base, entries):
        for slot, entry in enumerate(entries):
            product = block_product(vec_ref[(entry >> 14) & 255], ring_ref[base, slot])
            tile = entry & 255
            sum_ref[tile] = sum_ref[tile] + product

    def out_copy(ring_ref, half, base, first):
        return pltpu.make_async_copy(
            ring_ref.at[base], store_ref.at[pl.ds(first, BUILD_SLOTS)], sems.at[half, base])

    def pair_block(ring_ref, base, slot, entry, own_pairs):
        own = jnp.minimum(entry & 255, tiles - 1)
        partner = (entry >> 14) & 255
        shift_a = (((entry >> 8) & 3) - 1).astype(jnp.float32) * length_scale
        shift_b = (((entry >> 10) & 3) - 1).astype(jnp.float32) * length_scale
        shift_c = (((entry >> 12) & 3) - 1).astype(jnp.float32) * length_scale
        theirs = row_ref[partner]
        full = (16, size)
        their_a = jnp.broadcast_to(theirs[0:1] + shift_a, full)
        their_b = jnp.broadcast_to(theirs[1:2] + shift_b, full)
        their_c = jnp.broadcast_to(theirs[2:3] + shift_c, full)
        their_shield = jnp.broadcast_to(theirs[3:4], full)
        their_width = jnp.broadcast_to(theirs[4:5], full)
        for group in range(size // 16):
            rows = slice(16 * group, 16 * group + 16)

            def mine(c):
                return spread_ref[own, rows, c * size : (c + 1) * size]

            delta_a = their_a - mine(0)
            delta_b = their_b - mine(1)
            delta_c = their_c - mine(2)
            distance = delta_a * delta_a + delta_b * delta_b + delta_c * delta_c
            coulomb = lax.rsqrt(distance + mine(3) * their_shield)
            response = response_scale * jnp.exp2(distance / (mine(4) + their_width))
            if own_pairs:
                line = lax.broadcasted_iota(jnp.int32, full, 0) + 16 * group
                other = line != lax.broadcasted_iota(jnp.int32, full, 1)
                coulomb = jnp.where(other, coulomb, 0.0)
                response = jnp.where(other, response, 0.0)
            ring_ref[base, slot, rows, :] = coulomb.astype(jnp.bfloat16)
            ring_ref[base, slot, size + 16 * group : size + 16 * group + 16, :] = response.astype(jnp.bfloat16)

    span = 2 * BUILD_SLOTS

    def entries_at(first):
        return [list_ref[first + slot] for slot in range(BUILD_SLOTS)]

    def turns(first, last, own_pairs):
        def visit(turn, carry):
            base = lax.rem(turn, BUILD_RING)
            before = lax.rem(turn + BUILD_RING - 1, BUILD_RING)
            start = turn * span

            @pl.when(turn >= BUILD_RING)
            def _():
                out_copy(even_ref, 0, base, 0).wait()
                out_copy(odd_ref, 1, base, 0).wait()

            late = [
                jnp.where(turn > 0, list_ref[jnp.maximum(start - BUILD_SLOTS + slot, 0)], tiles)
                for slot in range(BUILD_SLOTS)
            ]
            even, odd = entries_at(start), entries_at(start + BUILD_SLOTS)
            multiply(odd_ref, before, late)
            for slot, entry in enumerate(even):
                pair_block(even_ref, base, slot, entry, own_pairs)
            multiply(even_ref, base, even)
            for slot, entry in enumerate(odd):
                pair_block(odd_ref, base, slot, entry, own_pairs)
            out_copy(even_ref, 0, base, start).start()
            out_copy(odd_ref, 1, base, start + BUILD_SLOTS).start()
            return carry

        lax.fori_loop(first, last, visit, 0)

    assert tiles % span == 0
    own_turns = tiles // span
    all_turns = (count + span - 1) // span
    turns(0, own_turns, True)
    turns(own_turns, all_turns, False)
    final = all_turns - 1
    multiply(odd_ref, lax.rem(final, BUILD_RING), entries_at(final * span + BUILD_SLOTS))
    for group in range(BUILD_RING):
        @pl.when(group < all_turns)
        def _():
            out_copy(even_ref, 0, group, 0).wait()
            out_copy(odd_ref, 1, group, 0).wait()

    def finish(tile, carry):
        total = sum_ref[tile]
        one = pl.ds(tile, 1)
        diag_charge = hard_ref[one, :] + total[12:13, 0:128] - SHIFT
        diag_potential = soft_ref[one, :] + total[12:13, 128:256] - SHIFT
        diag_charge_ref[one, :] = diag_charge
        diag_potential_ref[one, :] = diag_potential
        values = own_ref[pl.ds(tile, 4, stride=tiles), :]
        pair_charge, pair_potential = pair_parts(total)
        image_ref[pl.ds(tile, 4, stride=tiles), :] = image_rows(
            values, pair_charge, pair_potential, diag_charge, diag_potential, link_ref[one, :])
        return carry

    lax.fori_loop(0, tiles, finish, 0, unroll=4)


def apply_kernel(list_ref, count_ref, joined_ref, own_ref, diag_charge_ref, diag_potential_ref, link_ref,
                 store_ref, image_ref, vec_ref, sum_ref, ring_ref, sems):
    tiles = link_ref.shape[0]
    rows_all = vec_ref.shape[0]
    count = count_ref[0]
    turns = (count + APPLY_CHUNK - 1) // APPLY_CHUNK

    def in_copy(turn, first=0, places=APPLY_CHUNK):
        slot = lax.rem(turn, APPLY_RING)
        return pltpu.make_async_copy(
            store_ref.at[pl.ds(turn * APPLY_CHUNK + first, places)],
            ring_ref.at[slot, pl.ds(first, places)], sems.at[slot])

    def start_copies(turn):
        for first in range(0, APPLY_CHUNK, APPLY_COPY):
            in_copy(turn, first, APPLY_COPY).start()

    for turn in range(APPLY_RING - 1):
        @pl.when(turn < turns)
        def _():
            start_copies(turn)

    fill_vectors(joined_ref, 0, rows_all, vec_ref)

    def clear(tile, carry):
        sum_ref[tile] = jnp.zeros(sum_ref.shape[1:], jnp.float32)
        return carry

    lax.fori_loop(0, tiles + 1, clear, 0, unroll=4)

    def visit(turn, carry):
        slot = lax.rem(turn, APPLY_RING)

        @pl.when(turn + APPLY_RING - 1 < turns)
        def _():
            start_copies(turn + APPLY_RING - 1)

        in_copy(turn).wait()
        entries = [list_ref[turn * APPLY_CHUNK + place] for place in range(APPLY_CHUNK)]
        products = [
            block_product(vec_ref[(entry >> 14) & 255], ring_ref[slot, place])
            for place, entry in enumerate(entries)
        ]
        for entry, product in zip(entries, products):
            tile = entry & 255
            sum_ref[tile] = sum_ref[tile] + product
        return carry

    lax.fori_loop(0, turns, visit, 0)

    def finish(tile, carry):
        total = sum_ref[tile]
        one = pl.ds(tile, 1)
        values = own_ref[pl.ds(tile, 4, stride=tiles), :]
        pair_charge, pair_potential = pair_parts(total)
        image_ref[pl.ds(tile, 4, stride=tiles), :] = image_rows(
            values, pair_charge, pair_potential, diag_charge_ref[one, :], diag_potential_ref[one, :],
            link_ref[one, :])
        return carry

    lax.fori_loop(0, tiles, finish, 0, unroll=4)


def moment_kernel(zero_ref, one_ref, two_ref, three_ref, out_ref):
    tiles = zero_ref.shape[0] // 4
    refs = (zero_ref, one_ref, two_ref, three_ref)
    lane = lax.broadcasted_iota(jnp.int32, (1, 128), 1)
    for system in range(2):
        line = jnp.zeros((1, 128), jnp.float32)
        for degree in range(2 * ITERS):
            left, right = refs[degree // 2], refs[degree - degree // 2]
            low = slice(system * tiles, system * tiles + tiles)
            high = slice((2 + system) * tiles, (2 + system) * tiles + tiles)
            product = left[low, :] * right[low, :] + left[high, :] * right[high, :]
            line = jnp.where(lane == degree, jnp.sum(product, keepdims=True), line)
        out_ref[system : system + 1, :] = line


def combine_kernel(moments_ref, zero_ref, one_ref, two_ref, three_ref, solution_ref, residual_ref):
    tiles = zero_ref.shape[0] // 4
    total = jnp.sum(moments_ref[...], axis=0)
    moments = [total[:, degree : degree + 1] for degree in range(2 * ITERS)]

    def times(poly):
        grown = [SHIFT * c for c in poly] + [jnp.zeros_like(poly[0])]
        return [c + p for c, p in zip(grown, [jnp.zeros_like(poly[0])] + poly)]

    def product(left, right):
        out = 0.0
        for i, a in enumerate(left):
            for j, c in enumerate(right):
                out = out + a * c * moments[i + j]
        return out

    def axpy(left, scale, right):
        length = max(len(left), len(right))
        zero = jnp.zeros_like(scale)
        left = left + [zero] * (length - len(left))
        right = right + [zero] * (length - len(right))
        return [a + scale * c for a, c in zip(left, right)]

    one = jnp.ones_like(moments[0])
    found = [jnp.zeros_like(one)]
    rest = [one]
    direction = [one]
    norm = moments[0]
    for iteration in range(ITERS):
        along = times(direction)
        step = norm / product(direction, along)
        found = axpy(found, step, direction)
        rest = axpy(rest, -step, along)
        if iteration + 1 < ITERS:
            norm_next = product(rest, rest)
            direction = axpy(rest, norm_next / norm, direction)
            norm = norm_next
    refs = (zero_ref, one_ref, two_ref, three_ref)
    for field in range(4):
        system = field % 2
        span = slice(field * tiles, field * tiles + tiles)
        for poly, out_ref in ((found, solution_ref), (rest, residual_ref)):
            value = 0.0
            for c, ref in zip(poly, refs):
                value = value + c[system : system + 1, :] * ref[span, :]
            out_ref[span, :] = value


VMEM = pltpu.MemorySpace.VMEM
SMEM = pltpu.MemorySpace.SMEM


def in_vmem():
    return pl.BlockSpec(memory_space=VMEM)


def in_smem():
    return pl.BlockSpec(memory_space=SMEM)


def on_device(positions, shield, width, hardness, softness, coupling, pair_bits, right_side):
    extent = hardness.shape[:3]
    size = hardness.shape[3]
    tiles = extent[0] * extent[1] * extent[2]
    counts = {axis: lax.axis_size(axis) for axis in AXES}
    f32 = jnp.float32

    hard, soft, link = (a.reshape(tiles, size) for a in (hardness, softness, coupling))
    start = right_side.reshape(4, tiles, size)
    fields = jnp.concatenate(
        [positions.reshape(3, tiles, size), shield.reshape(1, tiles, size), width.reshape(1, tiles, size), start],
        axis=0)
    joined, boxes = extended(fields, extent)
    rows_all = joined.shape[1]
    table = candidate_table(boxes, extent, counts)
    capacity = table.shape[0] + max(2 * BUILD_SLOTS, APPLY_CHUNK)

    slots, count = pl.pallas_call(
        list_kernel,
        out_shape=(jax.ShapeDtypeStruct((capacity,), jnp.int32), jax.ShapeDtypeStruct((1,), jnp.int32)),
        in_specs=[in_smem(), in_smem()],
        out_specs=(in_smem(), in_smem()),
        name="pair_list",
    )(pair_bits.reshape(tiles), jnp.asarray(table))

    flat = (4 * tiles, size)
    start_flat = start.reshape(flat)
    store, diag_charge, diag_potential, image = pl.pallas_call(
        build_kernel,
        out_shape=(
            jax.ShapeDtypeStruct((capacity, 2 * size, size), jnp.bfloat16),
            jax.ShapeDtypeStruct((tiles, size), f32),
            jax.ShapeDtypeStruct((tiles, size), f32),
            jax.ShapeDtypeStruct(flat, f32),
        ),
        in_specs=[in_smem(), in_smem()] + [in_vmem()] * 5,
        out_specs=(pl.BlockSpec(memory_space=pl.ANY), in_vmem(), in_vmem(), in_vmem()),
        scratch_shapes=[
            pltpu.VMEM((rows_all, 8, size), f32),
            pltpu.VMEM((tiles, size, 5 * size), f32),
            pltpu.VMEM((rows_all, 16, size), jnp.bfloat16),
            pltpu.VMEM((tiles + 1, 16, 2 * size), f32),
            pltpu.VMEM((BUILD_RING, BUILD_SLOTS, 2 * size, size), jnp.bfloat16),
            pltpu.VMEM((BUILD_RING, BUILD_SLOTS, 2 * size, size), jnp.bfloat16),
            pltpu.SemaphoreType.DMA((2, BUILD_RING)),
        ],
        compiler_params=pltpu.CompilerParams(vmem_limit_bytes=40 * 2**20),
        name="build",
    )(slots, count, joined.reshape(-1, size), start_flat, hard, soft, link)

    def operate(vector):
        spread, _ = extended(vector.reshape(4, tiles, size), extent)
        return pl.pallas_call(
            apply_kernel,
            out_shape=jax.ShapeDtypeStruct(flat, f32),
            in_specs=[in_smem(), in_smem()] + [in_vmem()] * 5 + [pl.BlockSpec(memory_space=pl.ANY)],
            out_specs=in_vmem(),
            scratch_shapes=[
                pltpu.VMEM((rows_all, 16, size), jnp.bfloat16),
                pltpu.VMEM((tiles + 1, 16, 2 * size), f32),
                pltpu.VMEM((APPLY_RING, APPLY_CHUNK, 2 * size, size), jnp.bfloat16),
                pltpu.SemaphoreType.DMA((APPLY_RING,)),
            ],
            compiler_params=pltpu.CompilerParams(vmem_limit_bytes=40 * 2**20),
            name="apply",
        )(slots, count, spread.reshape(-1, size), vector, diag_charge, diag_potential, link, store)

    vectors = [start_flat, image]
    for _ in range(ITERS - 1):
        vectors.append(operate(vectors[-1]))

    moments = pl.pallas_call(
        moment_kernel,
        out_shape=jax.ShapeDtypeStruct((2, size), f32),
        in_specs=[in_vmem()] * 4,
        out_specs=in_vmem(),
        name="moments",
    )(*vectors)
    devices = counts["gx"] * counts["gy"] * counts["gz"]
    gathered = lax.all_to_all(jnp.broadcast_to(moments, (devices,) + moments.shape), AXES, 0, 0)
    solution, residual = pl.pallas_call(
        combine_kernel,
        out_shape=(jax.ShapeDtypeStruct(flat, f32), jax.ShapeDtypeStruct(flat, f32)),
        in_specs=[in_vmem()] * 5,
        out_specs=(in_vmem(), in_vmem()),
        name="combine",
    )(gathered, *vectors)
    return (solution.reshape(right_side.shape), residual.reshape(right_side.shape))


def solution(mesh):
    return jax.shard_map(
        on_device,
        mesh=mesh,
        in_specs=(
            P(None, "gx", "gy", "gz", None),
            P("gx", "gy", "gz", None),
            P("gx", "gy", "gz", None),
            P("gx", "gy", "gz", None),
            P("gx", "gy", "gz", None),
            P("gx", "gy", "gz", None),
            P("gx", "gy", "gz"),
            P(None, "gx", "gy", "gz", None),
        ),
        out_specs=(P(None, "gx", "gy", "gz", None), P(None, "gx", "gy", "gz", None)),
        check_vma=False,
    )
```

time: 629 us -> 136 us (0.22)
  other arithmetic: 283 us -> 2.86 us
  blocking collectives: 135 us -> 12 us
  matrix products: 106 us -> 0 us
  Pallas kernels: 0 us -> 61.6 us
  starting transfers between devices: 65.2 us -> 21.2 us
  waiting for transfers between devices: 16.2 us -> 25.4 us
    dynamic_update_slice x27 -> x0, other arithmetic: 141 us -> none  [build(): lax.dynamic_update_index_in_dim(store_response, response, offset_code, 0)]
    reduce_sum x38 -> x0, other arithmetic: 136 us -> none  [the longest x27 135 us: build(): row_response = row_response + jnp.sum(response.astype(jnp.float32), axis=2)]
    psum x3 -> x0, blocking collectives: 135 us -> none  [two_products(): lax.psum((inner_local(vector, vector), inner_local(vector, applied)), ('g...]
    dot_general x8 -> x0, matrix products: 106 us -> none  [the longest x4 53.5 us: operate(): jnp.einsum('otij,oftj->fti', store_coulomb, stacked[:, :4], preferred_ele...]
    pallas_call x0 -> x6, Pallas kernels: none -> 61.6 us  [the longest x1 28.8 us: on_device(): pl.pallas_call(build_kernel, out_shape=(jax.ShapeDtypeStruct((capacity, 2...]
    ppermute x24 -> x15, starting transfers between devices: 65.2 us -> 21.2 us  [the longest x6 9.53 us: extended(): low = lax.ppermute(last, axis, forward)]
    all_to_all x0 -> x1, blocking collectives: none -> 12 us  [on_device(): lax.all_to_all(jnp.broadcast_to(moments, (devices,) + moments.shape), AXE...]
    ppermute x24 -> x15, waiting for transfers between devices: 16.2 us -> 25.4 us  [the longest x6 10.1 us: extended(): low = lax.ppermute(last, axis, forward)]
  transfers between devices with their start and end apart: 24 -> 15, of which waited for: 16 -> 12; matrix products, arithmetic and copies ran while one was open for 0% -> 2% of each run, Pallas kernels for 0% -> 2%
where the time goes in v1:
time: 136 us; the launch traced here: 134 us
  Pallas kernels  61.6 us (45%)
  waiting for transfers between devices  25.4 us (19%)
  starting transfers between devices  21.2 us (16%)
  blocking collectives  12 us (9%)
  local copies, waits for them, and re-layouts  10.2 us (7%)
  other arithmetic  2.86 us (2%)
    pallas_call x1, Pallas kernels, on_device(): pl.pallas_call(build_kernel, out_shape=(jax.ShapeDtypeStruct((capacity, 2...  28.8 us
    pallas_call x2, Pallas kernels, operate(): pl.pallas_call(apply_kernel, out_shape=jax.ShapeDtypeStruct(flat, f32), i...  26.2 us
    all_to_all x1, blocking collectives, on_device(): lax.all_to_all(jnp.broadcast_to(moments, (devices,) + moments.shape), AXE...  12 us
    ppermute x6, waiting for transfers between devices, extended(): low = lax.ppermute(last, axis, forward)  10.1 us
    ppermute x6, starting transfers between devices, extended(): low = lax.ppermute(last, axis, forward)  9.53 us
    ppermute x6, starting transfers between devices, extended(): high = lax.ppermute(first, axis, backward)  9.3 us
    ppermute x3, waiting for transfers between devices, extended(): got = lax.ppermute(sent, axis, [(0, 1), (1, 0)])  9.27 us
    ppermute x6, waiting for transfers between devices, extended(): high = lax.ppermute(first, axis, backward)  5.97 us
  transfers between devices with their start and end apart: 15, of which 12 were waited for; matrix products, arithmetic and copies ran while one was open for 2% of the time, Pallas kernels for 2%

profile of v1, /device:TPU:0, one launch (start us, length us, event | category | flops | bytes accessed | tf_op | source)
XLA Modules:
  0.0 134.4 jit_solution(17416508825456770496)
XLA Ops:
  0.6 0.0 copy-start.6
  0.6 1.0 pad_maximum_fusion.8
  1.6 0.5 collective-permute-start
  2.2 2.0 %collective-permute-start.1 = (f32[9,4,128]{2,1,0:T(4,128)S(1)}, f32[9,4,128]{2,1,0:T(4,128)S(1)}, u32[]{:S(2)}, u32[]{:S(2)}) collective-permute-start(f32[9,4,128]{2,1,0:T(4,128)S(1)} %bitcast.290), channel_id=1, source_target_pairs={{1,0},{2,1},{3,2},{0,3},{5,4},{6,5},{7,6},{4,7},{9,8},{10,9},{11,1... | collective-permute-start | bytes 55304 | tf_op jit(solution)/shard_map/ppermute | solution.py:82
  4.2 0.9 pad_maximum_fusion.1
  5.1 0.5 collective-permute-done
  5.6 0.0 collective-permute-done.1
  5.7 2.4 %collective-permute-start.2 = (f32[9,20,128]{2,1,0:T(8,128)S(1)}, f32[9,20,128]{2,1,0:T(8,128)S(1)}, u32[]{:S(2)}, u32[]{:S(2)}) collective-permute-start(f32[9,20,128]{2,1,0:T(8,128)S(1)} %pad_maximum_fusion.2), channel_id=1, source_target_pairs={{0,8},{8,16},{16,24},{24,0},{1,9},{9,17},{17,25},{25,1},{2,10},{10... | collective-permute-start | bytes 276488 | tf_op jit(solution)/shard_map/ppermute | solution.py:81
  8.1 2.1 %collective-permute-start.3 = (f32[9,20,128]{2,1,0:T(8,128)S(1)}, f32[9,20,128]{2,1,0:T(8,128)S(1)}, u32[]{:S(2)}, u32[]{:S(2)}) collective-permute-start(f32[9,20,128]{2,1,0:T(8,128)S(1)} %pad_maximum_fusion.3), channel_id=1, source_target_pairs={{8,0},{16,8},{24,16},{0,24},{9,1},{17,9},{25,17},{1,25},{10,2},{18... | collective-permute-start | bytes 276488 | tf_op jit(solution)/shard_map/ppermute | solution.py:82
  10.2 3.1 %collective-permute-done.2 = f32[9,20,128]{2,1,0:T(8,128)S(1)} collective-permute-done((f32[9,20,128]{2,1,0:T(8,128)S(1)}, f32[9,20,128]{2,1,0:T(8,128)S(1)}, u32[]{:S(2)}, u32[]{:S(2)}) %collective-permute-start.2) | collective-permute-done | bytes 92192 | tf_op jit(solution)/shard_map/ppermute | solution.py:81
  13.3 3.0 %collective-permute-done.3 = f32[9,20,128]{2,1,0:T(8,128)S(1)} collective-permute-done((f32[9,20,128]{2,1,0:T(8,128)S(1)}, f32[9,20,128]{2,1,0:T(8,128)S(1)}, u32[]{:S(2)}, u32[]{:S(2)}) %collective-permute-start.3) | collective-permute-done | bytes 92192 | tf_op jit(solution)/shard_map/ppermute | solution.py:82
  16.4 0.3 concatenate.62
  16.7 0.3 concatenate.61
  17.1 1.4 %collective-permute-start.4 = (f32[9,40,128]{2,1,0:T(8,128)S(1)}, f32[9,40,128]{2,1,0:T(8,128)S(1)}, u32[]{:S(2)}, u32[]{:S(2)}) collective-permute-start(f32[9,40,128]{2,1,0:T(8,128)S(1)} %broadcast_select_fusion), channel_id=1, source_target_pairs={{0,4},{4,0},{1,5},{5,1},{2,6},{6,2},{3,7},{7,3},{8,12},{12,8},{9,1... | collective-permute-start | bytes 552968 | tf_op jit(solution)/shard_map/ppermute | solution.py:76
  18.5 1.3 reshape.405.bits_ref
  19.8 3.1 %pair_list.1 = (s32[872]{0:T(1024)}, s32[1]{0:T(128)}) custom-call(s32[32]{0:T(128)} %reshape.405.bits_ref, s32[864]{0:T(1024)} %constant.10.clone.table_ref), custom_call_target="tpu_custom_call" | custom-call | tf_op jit(solution)/shard_map/pair_list/pallas_call | solution.py:479
  22.8 0.0 copy-start.9
  22.9 0.9 pad_maximum_fusion
  23.7 0.1 collective-permute-done.4
  23.8 0.2 concatenate.63
  24.0 0.0 copy-start.2
  24.0 0.8 copy-done.2
  24.9 0.7 copy-done.4
  25.6 0.7 copy-done.7
  26.3 0.7 copy-done.10
  27.0 0.7 copy-done.11
  27.7 28.8 %build.1 = (bf16[872,256,128]{2,1,0:T(8,128)(2,1)}, f32[32,128]{1,0:T(8,128)S(1)}, f32[32,128]{1,0:T(8,128)S(1)}, f32[128,128]{1,0:T(8,128)S(1)}) custom-call(s32[872]{0:T(1024)S(1)} %copy-done.7, s32[1]{0:T(128)} %get-tuple-element.11.count_ref, f32[1080,128]{1,0:T(8,128)S(1)} %bitcast.249, f32[128,128]{1,0:T(8,128)S(1)} %bitcast.248, ...), custom_call_target="tpu_custom_call" | custom-call | tf_op jit(solution)/shard_map/build/pallas_call | solution.py:489
  56.6 0.1 collective-permute-start.5
  56.7 1.7 %collective-permute-start.6 = (f32[4,4,128]{2,1,0:T(4,128)S(1)}, f32[4,4,128]{2,1,0:T(4,128)S(1)}, u32[]{:S(2)}, u32[]{:S(2)}) collective-permute-start(f32[4,4,128]{2,1,0:T(4,128)S(1)} %bitcast.305), channel_id=1, source_target_pairs={{1,0},{2,1},{3,2},{0,3},{5,4},{6,5},{7,6},{4,7},{9,8},{10,9},{11,1... | collective-permute-start | bytes 24584 | tf_op jit(solution)/shard_map/ppermute | solution.py:82
  58.4 1.3 collective-permute-done.5
  59.7 0.0 collective-permute-done.6
  59.8 4.2 %collective-permute-start.7 = (f32[4,20,128]{2,1,0:T(8,128)S(1)}, f32[4,20,128]{2,1,0:T(8,128)S(1)}, u32[]{:S(2)}, u32[]{:S(2)}) collective-permute-start(f32[4,20,128]{2,1,0:T(8,128)S(1)} %pad_maximum_fusion.4), channel_id=1, source_target_pairs={{0,8},{8,16},{16,24},{24,0},{1,9},{9,17},{17,25},{25,1},{2,10},{10... | collective-permute-start | bytes 122888 | tf_op jit(solution)/shard_map/ppermute | solution.py:81
  64.0 0.1 collective-permute-start.8
  64.1 2.0 %collective-permute-done.7 = f32[4,20,128]{2,1,0:T(8,128)S(1)} collective-permute-done((f32[4,20,128]{2,1,0:T(8,128)S(1)}, f32[4,20,128]{2,1,0:T(8,128)S(1)}, u32[]{:S(2)}, u32[]{:S(2)}) %collective-permute-start.7) | collective-permute-done | bytes 40992 | tf_op jit(solution)/shard_map/ppermute | solution.py:81
  66.1 2.0 %collective-permute-done.8 = f32[4,20,128]{2,1,0:T(8,128)S(1)} collective-permute-done((f32[4,20,128]{2,1,0:T(8,128)S(1)}, f32[4,20,128]{2,1,0:T(8,128)S(1)}, u32[]{:S(2)}, u32[]{:S(2)}) %collective-permute-start.8) | collective-permute-done | bytes 40992 | tf_op jit(solution)/shard_map/ppermute | solution.py:82
  68.2 0.2 concatenate.67
  68.5 0.2 concatenate.66
  68.7 0.3 collective-permute-start.9
  69.1 5.1 %collective-permute-done.9 = f32[4,40,128]{2,1,0:T(8,128)S(1)} collective-permute-done((f32[4,40,128]{2,1,0:T(8,128)S(1)}, f32[4,40,128]{2,1,0:T(8,128)S(1)}, u32[]{:S(2)}, u32[]{:S(2)}) %collective-permute-start.9) | collective-permute-done | bytes 81952 | tf_op jit(solution)/shard_map/ppermute | solution.py:76
  74.1 0.2 concatenate.68
  74.3 0.0 copy-start.5
  74.3 0.7 copy-done.5
  75.0 0.7 copy-done.8
  75.7 13.1 %apply.2.own_ref.two_ref = f32[128,128]{1,0:T(8,128)S(1)} custom-call(s32[872]{0:T(1024)S(1)} %copy-done.8, s32[1]{0:T(128)} %get-tuple-element.11.count_ref, f32[480,128]{1,0:T(8,128)S(1)} %bitcast.251, f32[128,128]{1,0:T(8,128)S(1)} %get-tuple-element.12.own_ref.one_ref, f32[32,128]{1,0:T(8,128)S(1)} %get-tuple-element.13.diag_charge_ref, ...), custom_call_target="tpu_custom_call" | custom-call | tf_op jit(solution)/shard_map/apply/pallas_call | solution.py:514
  88.8 0.0 copy-start
  88.8 0.2 collective-permute-start.10
  89.0 1.6 %collective-permute-start.11 = (f32[4,4,128]{2,1,0:T(4,128)S(1)}, f32[4,4,128]{2,1,0:T(4,128)S(1)}, u32[]{:S(2)}, u32[]{:S(2)}) collective-permute-start(f32[4,4,128]{2,1,0:T(4,128)S(1)} %bitcast.304), channel_id=1, source_target_pairs={{1,0},{2,1},{3,2},{0,3},{5,4},{6,5},{7,6},{4,7},{9,8},{10,9},{11,1... | collective-permute-start | bytes 24584 | tf_op jit(solution)/shard_map/ppermute | solution.py:82
  90.7 1.3 collective-permute-done.10
  92.0 0.0 collective-permute-done.11
  92.0 2.1 %collective-permute-start.12 = (f32[4,20,128]{2,0,1:T(4,128)S(1)}, f32[4,20,128]{2,0,1:T(4,128)S(1)}, u32[]{:S(2)}, u32[]{:S(2)}) collective-permute-start(f32[4,20,128]{2,0,1:T(4,128)S(1)} %pad_maximum_fusion.6), channel_id=1, source_target_pairs={{0,8},{8,16},{16,24},{24,0},{1,9},{9,17},{17,25},{25,1},{2,10},{10... | collective-permute-start | bytes 122888 | tf_op jit(solution)/shard_map/ppermute | solution.py:81
  94.2 1.8 %collective-permute-start.13 = (f32[4,20,128]{2,0,1:T(4,128)S(1)}, f32[4,20,128]{2,0,1:T(4,128)S(1)}, u32[]{:S(2)}, u32[]{:S(2)}) collective-permute-start(f32[4,20,128]{2,0,1:T(4,128)S(1)} %pad_maximum_fusion.7), channel_id=1, source_target_pairs={{8,0},{16,8},{24,16},{0,24},{9,1},{17,9},{25,17},{1,25},{10,2},{18... | collective-permute-start | bytes 122888 | tf_op jit(solution)/shard_map/ppermute | solution.py:82
  96.0 2.0 %collective-permute-done.12 = f32[4,20,128]{2,0,1:T(4,128)S(1)} collective-permute-done((f32[4,20,128]{2,0,1:T(4,128)S(1)}, f32[4,20,128]{2,0,1:T(4,128)S(1)}, u32[]{:S(2)}, u32[]{:S(2)}) %collective-permute-start.12) | collective-permute-done | bytes 40992 | tf_op jit(solution)/shard_map/ppermute | solution.py:81
  98.1 0.8 collective-permute-done.13
  98.9 0.2 concatenate.72
  99.2 0.2 concatenate.71
  99.4 0.6 collective-permute-start.14
  100.1 4.2 %collective-permute-done.14 = f32[4,40,128]{2,1,0:T(8,128)S(1)} collective-permute-done((f32[4,40,128]{2,1,0:T(8,128)S(1)}, f32[4,40,128]{2,1,0:T(8,128)S(1)}, u32[]{:S(2)}, u32[]{:S(2)}) %collective-permute-start.14) | collective-permute-done | bytes 81952 | tf_op jit(solution)/shard_map/ppermute | solution.py:76
  104.2 0.2 concatenate.73
  104.4 13.1 %apply.3.three_ref = f32[128,128]{1,0:T(8,128)S(1)} custom-call(s32[872]{0:T(1024)S(1)} %copy-done.9, s32[1]{0:T(128)} %get-tuple-element.11.count_ref, f32[480,128]{1,0:T(8,128)S(1)} %bitcast.250, f32[128,128]{1,0:T(8,128)S(1)} %apply.2.own_ref.two_ref, f32[32,128]{1,0:T(8,128)S(1)} %get-tuple-element.13.diag_charge_ref, ...), custom_call_target="tpu_custom_call" | custom-call | tf_op jit(solution)/shard_map/apply/pallas_call | solution.py:514
  117.6 0.6 copy-done.3
  118.2 1.6 %moments.1 = f32[2,128]{1,0:T(2,128)} custom-call(f32[128,128]{1,0:T(8,128)} %bitcast.246, f32[128,128]{1,0:T(8,128)} %copy-done.1, f32[128,128]{1,0:T(8,128)} %copy-done, f32[128,128]{1,0:T(8,128)} %copy-done.3), custom_call_target="tpu_custom_call" | custom-call | tf_op jit(solution)/shard_map/moments/pallas_call | solution.py:533
  119.8 0.7 broadcast_in_dim.3
  120.5 12.0 %all_to_all.5.moments_ref = f32[32,2,128]{2,1,0:T(2,128)} all-to-all(f32[32,2,128]{2,1,0:T(2,128)S(1)} %broadcast_in_dim.3), channel_id=1, replica_groups=mesh['gx'=4,'gy'=2,'gz'=4] {'gx','gy','gz'}, dimensions={0} | all-to-all | bytes 65536 | tf_op jit(solution)/shard_map/all_to_all | solution.py:541
  132.5 1.8 %combine.1 = (f32[128,128]{1,0:T(8,128)}, f32[128,128]{1,0:T(8,128)}) custom-call(f32[32,2,128]{2,1,0:T(2,128)} %all_to_all.5.moments_ref, f32[128,128]{1,0:T(8,128)} %bitcast.247, f32[128,128]{1,0:T(8,128)} %copy-done.1, f32[128,128]{1,0:T(8,128)} %copy-done, f32[128,128]{1,0:T(8,128)} %copy-done.3), custom_call_target="tpu_custom_call" | custom-call | tf_op jit(solution)/shard_map/combine/pallas_call | solution.py:542
  (82 shorter events, 0.5 us)
Async XLA Ops:
  0.6 103.8 %copy-start.6 = (f32[2,2,8,128]{3,2,1,0:T(8,128)S(1)}, f32[2,2,8,128]{3,2,1,0:T(8,128)}, u32[]{:S(2)}) copy-start(f32[2,2,8,128]{3,2,1,0:T(8,128)} %param.14) | copy-start | bytes 49156
  1.6 3.9 %collective-permute-start = (f32[9,4,128]{2,1,0:T(4,128)S(1)}, f32[9,4,128]{2,1,0:T(4,128)S(1)}, u32[]{:S(2)}, u32[]{:S(2)}) collective-permute-start(f32[9,4,128]{2,1,0:T(4,128)S(1)} %bitcast.291), channel_id=1, source_target_pairs={{0,1},{1,2},{2,3},{3,0},{4,5},{5,6},{6,7},{7,4},{8,9},{9,10},{10,1... | collective-permute-start | bytes 55304 | tf_op jit(solution)/shard_map/ppermute | solution.py:81
  2.2 3.4 %collective-permute-start.1 = (f32[9,4,128]{2,1,0:T(4,128)S(1)}, f32[9,4,128]{2,1,0:T(4,128)S(1)}, u32[]{:S(2)}, u32[]{:S(2)}) collective-permute-start(f32[9,4,128]{2,1,0:T(4,128)S(1)} %bitcast.290), channel_id=1, source_target_pairs={{1,0},{2,1},{3,2},{0,3},{5,4},{6,5},{7,6},{4,7},{9,8},{10,9},{11,1... | collective-permute-start | bytes 55304 | tf_op jit(solution)/shard_map/ppermute | solution.py:82
  5.7 7.6 %collective-permute-start.2 = (f32[9,20,128]{2,1,0:T(8,128)S(1)}, f32[9,20,128]{2,1,0:T(8,128)S(1)}, u32[]{:S(2)}, u32[]{:S(2)}) collective-permute-start(f32[9,20,128]{2,1,0:T(8,128)S(1)} %pad_maximum_fusion.2), channel_id=1, source_target_pairs={{0,8},{8,16},{16,24},{24,0},{1,9},{9,17},{17,25},{25,1},{2,10},{10... | collective-permute-start | bytes 276488 | tf_op jit(solution)/shard_map/ppermute | solution.py:81
  8.1 8.3 %collective-permute-start.3 = (f32[9,20,128]{2,1,0:T(8,128)S(1)}, f32[9,20,128]{2,1,0:T(8,128)S(1)}, u32[]{:S(2)}, u32[]{:S(2)}) collective-permute-start(f32[9,20,128]{2,1,0:T(8,128)S(1)} %pad_maximum_fusion.3), channel_id=1, source_target_pairs={{8,0},{16,8},{24,16},{0,24},{9,1},{17,9},{25,17},{1,25},{10,2},{18... | collective-permute-start | bytes 276488 | tf_op jit(solution)/shard_map/ppermute | solution.py:82
  17.1 6.7 %collective-permute-start.4 = (f32[9,40,128]{2,1,0:T(8,128)S(1)}, f32[9,40,128]{2,1,0:T(8,128)S(1)}, u32[]{:S(2)}, u32[]{:S(2)}) collective-permute-start(f32[9,40,128]{2,1,0:T(8,128)S(1)} %broadcast_select_fusion), channel_id=1, source_target_pairs={{0,4},{4,0},{1,5},{5,1},{2,6},{6,2},{3,7},{7,3},{8,12},{12,8},{9,1... | collective-permute-start | bytes 552968 | tf_op jit(solution)/shard_map/ppermute | solution.py:76
  22.8 81.6 %copy-start.9 = (s32[872]{0:T(1024)S(1)}, s32[872]{0:T(1024)}, u32[]{:S(2)}) copy-start(s32[872]{0:T(1024)} %get-tuple-element.10.list_ref) | copy-start | bytes 10468
  24.0 0.8 copy-start.2
  24.9 0.7 copy-start.4
  25.6 0.7 copy-start.7
  26.3 0.7 copy-start.10
  27.0 0.7 copy-start.11
  56.5 61.0 %copy-start.1 = (f32[128,128]{1,0:T(8,128)}, f32[128,128]{1,0:T(8,128)S(1)}, u32[]{:S(2)}) copy-start(f32[128,128]{1,0:T(8,128)S(1)} %get-tuple-element.12.own_ref.one_ref) | copy-start | bytes 196612
  56.6 3.1 %collective-permute-start.5 = (f32[4,4,128]{2,1,0:T(4,128)S(1)}, f32[4,4,128]{2,1,0:T(4,128)S(1)}, u32[]{:S(2)}, u32[]{:S(2)}) collective-permute-start(f32[4,4,128]{2,1,0:T(4,128)S(1)} %bitcast.307), channel_id=1, source_target_pairs={{0,1},{1,2},{2,3},{3,0},{4,5},{5,6},{6,7},{7,4},{8,9},{9,10},{10,1... | collective-permute-start | bytes 24584 | tf_op jit(solution)/shard_map/ppermute | solution.py:81
  56.7 3.1 %collective-permute-start.6 = (f32[4,4,128]{2,1,0:T(4,128)S(1)}, f32[4,4,128]{2,1,0:T(4,128)S(1)}, u32[]{:S(2)}, u32[]{:S(2)}) collective-permute-start(f32[4,4,128]{2,1,0:T(4,128)S(1)} %bitcast.305), channel_id=1, source_target_pairs={{1,0},{2,1},{3,2},{0,3},{5,4},{6,5},{7,6},{4,7},{9,8},{10,9},{11,1... | collective-permute-start | bytes 24584 | tf_op jit(solution)/shard_map/ppermute | solution.py:82
  59.8 6.3 %collective-permute-start.7 = (f32[4,20,128]{2,1,0:T(8,128)S(1)}, f32[4,20,128]{2,1,0:T(8,128)S(1)}, u32[]{:S(2)}, u32[]{:S(2)}) collective-permute-start(f32[4,20,128]{2,1,0:T(8,128)S(1)} %pad_maximum_fusion.4), channel_id=1, source_target_pairs={{0,8},{8,16},{16,24},{24,0},{1,9},{9,17},{17,25},{25,1},{2,10},{10... | collective-permute-start | bytes 122888 | tf_op jit(solution)/shard_map/ppermute | solution.py:81
  64.0 4.1 %collective-permute-start.8 = (f32[4,20,128]{2,1,0:T(8,128)S(1)}, f32[4,20,128]{2,1,0:T(8,128)S(1)}, u32[]{:S(2)}, u32[]{:S(2)}) collective-permute-start(f32[4,20,128]{2,1,0:T(8,128)S(1)} %pad_maximum_fusion.5), channel_id=1, source_target_pairs={{8,0},{16,8},{24,16},{0,24},{9,1},{17,9},{25,17},{1,25},{10,2},{18... | collective-permute-start | bytes 122888 | tf_op jit(solution)/shard_map/ppermute | solution.py:82
  68.7 5.4 %collective-permute-start.9 = (f32[4,40,128]{2,1,0:T(8,128)S(1)}, f32[4,40,128]{2,1,0:T(8,128)S(1)}, u32[]{:S(2)}, u32[]{:S(2)}) collective-permute-start(f32[4,40,128]{2,1,0:T(8,128)S(1)} %broadcast_select_fusion.2), channel_id=1, source_target_pairs={{0,4},{4,0},{1,5},{5,1},{2,6},{6,2},{3,7},{7,3},{8,12},{12,8},{9,1... | collective-permute-start | bytes 245768 | tf_op jit(solution)/shard_map/ppermute | solution.py:76
  74.3 0.7 copy-start.5
  75.0 0.7 copy-start.8
  88.8 28.8 %copy-start = (f32[128,128]{1,0:T(8,128)}, f32[128,128]{1,0:T(8,128)S(1)}, u32[]{:S(2)}) copy-start(f32[128,128]{1,0:T(8,128)S(1)} %apply.2.own_ref.two_ref) | copy-start | bytes 196612
  88.8 3.1 %collective-permute-start.10 = (f32[4,4,128]{2,1,0:T(4,128)S(1)}, f32[4,4,128]{2,1,0:T(4,128)S(1)}, u32[]{:S(2)}, u32[]{:S(2)}) collective-permute-start(f32[4,4,128]{2,1,0:T(4,128)S(1)} %bitcast.306), channel_id=1, source_target_pairs={{0,1},{1,2},{2,3},{3,0},{4,5},{5,6},{6,7},{7,4},{8,9},{9,10},{10,1... | collective-permute-start | bytes 24584 | tf_op jit(solution)/shard_map/ppermute | solution.py:81
  89.0 3.0 %collective-permute-start.11 = (f32[4,4,128]{2,1,0:T(4,128)S(1)}, f32[4,4,128]{2,1,0:T(4,128)S(1)}, u32[]{:S(2)}, u32[]{:S(2)}) collective-permute-start(f32[4,4,128]{2,1,0:T(4,128)S(1)} %bitcast.304), channel_id=1, source_target_pairs={{1,0},{2,1},{3,2},{0,3},{5,4},{6,5},{7,6},{4,7},{9,8},{10,9},{11,1... | collective-permute-start | bytes 24584 | tf_op jit(solution)/shard_map/ppermute | solution.py:82
  92.0 6.0 %collective-permute-start.12 = (f32[4,20,128]{2,0,1:T(4,128)S(1)}, f32[4,20,128]{2,0,1:T(4,128)S(1)}, u32[]{:S(2)}, u32[]{:S(2)}) collective-permute-start(f32[4,20,128]{2,0,1:T(4,128)S(1)} %pad_maximum_fusion.6), channel_id=1, source_target_pairs={{0,8},{8,16},{16,24},{24,0},{1,9},{9,17},{17,25},{25,1},{2,10},{10... | collective-permute-start | bytes 122888 | tf_op jit(solution)/shard_map/ppermute | solution.py:81
  94.2 4.6 %collective-permute-start.13 = (f32[4,20,128]{2,0,1:T(4,128)S(1)}, f32[4,20,128]{2,0,1:T(4,128)S(1)}, u32[]{:S(2)}, u32[]{:S(2)}) collective-permute-start(f32[4,20,128]{2,0,1:T(4,128)S(1)} %pad_maximum_fusion.7), channel_id=1, source_target_pairs={{8,0},{16,8},{24,16},{0,24},{9,1},{17,9},{25,17},{1,25},{10,2},{18... | collective-permute-start | bytes 122888 | tf_op jit(solution)/shard_map/ppermute | solution.py:82
  99.4 4.8 %collective-permute-start.14 = (f32[4,40,128]{2,1,0:T(8,128)S(1)}, f32[4,40,128]{2,1,0:T(8,128)S(1)}, u32[]{:S(2)}, u32[]{:S(2)}) collective-permute-start(f32[4,40,128]{2,1,0:T(8,128)S(1)} %broadcast_select_fusion.1), channel_id=1, source_target_pairs={{0,4},{4,0},{1,5},{5,1},{2,6},{6,2},{3,7},{7,3},{8,12},{12,8},{9,1... | collective-permute-start | bytes 245768 | tf_op jit(solution)/shard_map/ppermute | solution.py:76
  117.6 0.6 copy-start.3

commit v2 on v1

v2 whole, which is shorter than its diff:
```python
import functools
import math

import jax
import jax.numpy as jnp
import numpy as np
from jax import lax
from jax.experimental import pallas as pl
from jax.experimental.pallas import tpu as pltpu
from jax.sharding import PartitionSpec as P

ITERS = 3

coulomb_scale = 0.002
response_scale = 0.003
length_scale = 1.0 / coulomb_scale
width_scale = -math.log(2.0) * length_scale * length_scale

SHIFT = 3.0

AXES = ("gx", "gy", "gz")
HALO_ORDER = (("gy", 1), ("gx", 0), ("gz", 2))
PARTS = 3
TURN_BITS = 3
TURN = 1 << TURN_BITS
BUILD_SLOTS = TURN // 2
BUILD_PAIRS = BUILD_SLOTS // 2
BUILD_RING = 8
APPLY_COPY = 1
APPLY_RING = 10


class Piece:
    def __init__(self, array, boxes):
        self.array = array
        self.boxes = boxes

    def face(self, dim, level):
        rows, boxes = [], []
        offset = 0
        for origin, shape in self.boxes:
            volume = shape[0] * shape[1] * shape[2]
            if origin[dim] <= level < origin[dim] + shape[dim]:
                part = self.array[:, offset : offset + volume]
                part = part.reshape((part.shape[0],) + shape + part.shape[2:])
                part = lax.slice_in_dim(part, level - origin[dim], level - origin[dim] + 1, axis=dim + 1)
                cut = tuple(1 if d == dim else shape[d] for d in range(3))
                rows.append(part.reshape(part.shape[0], -1, part.shape[-1]))
                boxes.append((tuple(level if d == dim else origin[d] for d in range(3)), cut))
            offset += volume
        return rows, boxes


def whole_face(pieces, dim, level):
    rows, boxes = [], []
    for piece in pieces:
        more_rows, more_boxes = piece.face(dim, level)
        rows += more_rows
        boxes += more_boxes
    return (jnp.concatenate(rows, axis=1) if len(rows) > 1 else rows[0]), boxes


def moved(boxes, dim, level):
    return [(tuple(level if d == dim else o[d] for d in range(3)), s) for o, s in boxes]


def extended(block, extent):
    pieces = [Piece(block, [((0, 0, 0), extent)])]
    for axis, dim in HALO_ORDER:
        count = lax.axis_size(axis)
        if count == 1:
            continue
        size = extent[dim]
        first, boxes = whole_face(pieces, dim, 0)
        last, _ = whole_face(pieces, dim, size - 1)
        if count == 2:
            sent = jnp.where(lax.axis_index(axis) == 0, last, first)
            got = lax.ppermute(sent, axis, [(0, 1), (1, 0)])
            pieces = pieces + [Piece(got, moved(boxes, dim, size))]
        else:
            forward = [(i, (i + 1) % count) for i in range(count)]
            backward = [(target, source) for source, target in forward]
            low = lax.ppermute(last, axis, forward)
            high = lax.ppermute(first, axis, backward)
            pieces = pieces + [
                Piece(low, moved(boxes, dim, -1)),
                Piece(high, moved(boxes, dim, size)),
            ]
    joined = jnp.concatenate([piece.array for piece in pieces], axis=1)
    return joined, [box for piece in pieces for box in piece.boxes]


def storage_rows(boxes, extent, counts):
    rows = {}
    offset = 0
    for origin, shape in boxes:
        for a in range(shape[0]):
            for b in range(shape[1]):
                for c in range(shape[2]):
                    rows[(origin[0] + a, origin[1] + b, origin[2] + c)] = offset
                    offset += 1

    def row_of(coord):
        fixed = list(coord)
        for axis, dim in HALO_ORDER:
            outside = not 0 <= fixed[dim] < extent[dim]
            if outside and counts[axis] == 1:
                fixed[dim] = 0
            elif outside and counts[axis] == 2:
                fixed[dim] = extent[dim]
        return rows[tuple(fixed)]

    return row_of


def candidate_pairs(boxes, extent, counts):
    row_of = storage_rows(boxes, extent, counts)
    tiles = extent[0] * extent[1] * extent[2]
    halo, inner = [], []
    for x in range(extent[0]):
        for y in range(extent[1]):
            for z in range(extent[2]):
                own = (x * extent[1] + y) * extent[2] + z
                halo.append([])
                inner.append([])
                for code in range(27):
                    a, b, c = code // 9, code // 3 % 3, code % 3
                    partner = row_of((x + a - 1, y + b - 1, z + c - 1))
                    assert own < 255 and partner < 255
                    entry = packed(own, partner, a, b, c)
                    if partner >= tiles:
                        halo[-1].append((code, entry))
                    elif partner > own:
                        inner[-1].append((code, entry))
    return halo, inner


def packed(own, partner, a=1, b=1, c=1):
    return own | a << 8 | b << 10 | c << 12 | partner << 14


def own_of(entry):
    return entry & 255


def partner_of(entry):
    return (entry >> 14) & 255


def list_table(found_of, never):
    longest = max(len(found) for found in found_of)
    table = [
        [entry | code << 22 for code, entry in found] + [never | 31 << 22] * (longest - len(found))
        for found in found_of
    ]
    return np.asarray([entry - (1 << 32) if entry >> 31 else entry for row in table for entry in row], np.int32)


def list_kernel(bits_ref, halo_ref, inner_ref, list_ref, word_ref, *, spare):
    height, depth = bits_ref.shape[1:]
    tiles = word_ref.shape[0]
    for tile in range(tiles):
        list_ref[tile] = jnp.int32(packed(tile, tile))
        word_ref[tile] = bits_ref[tile // (height * depth), tile // depth % height, tile % depth]
    filled = jnp.int32(tiles)
    for part, table_ref in enumerate((halo_ref, inner_ref)):
        longest = table_ref.shape[0] // tiles

        def visit(tile, filled):
            word = word_ref[tile]
            for place in range(longest):
                entry = table_ref[tile * longest + place]
                list_ref[filled] = entry
                filled = filled + ((word >> ((entry >> 22) & 31)) & 1)
            list_ref[filled] = tile | packed(0, spare)
            return filled + (filled & 1)

        filled = lax.fori_loop(0, tiles, visit, filled)

        def pad(extra, carry):
            list_ref[filled + extra] = jnp.int32(packed(tiles, spare))
            return carry

        lax.fori_loop(0, TURN, pad, 0)
        filled = (filled + TURN - 1) & -TURN
        list_ref[list_ref.shape[0] - 2 + part] = filled >> TURN_BITS


def split_rows(values):
    parts = []
    rest = values
    for _ in range(PARTS):
        part = rest.astype(jnp.bfloat16).astype(jnp.float32)
        parts.append(part)
        rest = rest - part
    return parts


def fill_vectors(source_ref, first_row, rows_all, vec_ref):
    vec_ref[rows_all] = jnp.zeros(vec_ref.shape[1:], jnp.bfloat16)

    def one(tile, carry):
        values = source_ref[pl.ds(first_row + tile, 4, stride=rows_all), :]
        parts = split_rows(values)
        stacked = jnp.concatenate(parts + [jnp.ones_like(values)], axis=0)
        vec_ref[tile] = stacked.astype(jnp.bfloat16)
        return carry

    lax.fori_loop(0, rows_all, one, 0, unroll=8)


def pair_parts(total):
    joined = total[0:4] + total[4:8] + total[8:12]
    return joined[0:2, 0:128], joined[2:4, 128:256]


def image_rows(values, pair_charge, pair_potential, diag_charge, diag_potential, linking):
    charge, potential = values[0:2], values[2:4]
    image_charge = diag_charge * charge + pair_charge + linking * potential
    image_potential = diag_potential * potential - pair_potential + linking * charge
    return jnp.concatenate([image_charge, image_potential], axis=0)


def add_products(vec_ref, sum_ref, blocks, entries, kind):
    spare_sum = sum_ref.shape[0] - 1
    added = []

    def times(vectors, block):
        return jnp.dot(vectors, block, preferred_element_type=jnp.float32)

    for place, block in enumerate(blocks):
        pair = entries[2 * place : 2 * place + 2]
        half = block().shape[0] // 2
        if kind == "own":
            for side, entry in enumerate(pair):
                vectors = vec_ref[own_of(entry)]
                lanes = slice(side * half, side * half + half)
                added.append((own_of(entry), lax.dot_general(
                    vectors, block()[:, lanes], (((1,), (1,)), ((), ())), preferred_element_type=jnp.float32)))
            continue
        vectors = jnp.concatenate([vec_ref[partner_of(entry)] for entry in pair], axis=1)
        added.append((own_of(pair[0]), lax.dot_general(
            vectors, block(), (((1,), (1,)), ((), ())), preferred_element_type=jnp.float32)))
        if kind == "inner":
            vectors = vec_ref[own_of(pair[0])]
            coulomb, response = times(vectors, block()[:half]), times(vectors, block()[half:])
            for side, entry in enumerate(pair):
                lanes = slice(side * half, side * half + half)
                added.append((
                    jnp.minimum(partner_of(entry), spare_sum),
                    jnp.concatenate([coulomb[:, lanes], response[:, lanes]], axis=1)))
    for tile, product in added:
        sum_ref[tile] = sum_ref[tile] + product


def build_kernel(list_hbm, joined_ref, hard_hbm, soft_hbm, link_hbm,
                 store_ref, diag_ref, image_ref,
                 row_ref, spread_ref, vec_ref, sum_ref, even_ref, odd_ref,
                 local_ref, list_ref, apart_ref, sems, local_sems):
    tiles, size = hard_hbm.shape
    rows_all = vec_ref.shape[0] - 1

    def local_copies():
        return [
            pltpu.make_async_copy(source, local_ref.at[place], local_sems.at[place])
            for place, source in enumerate((hard_hbm, soft_hbm, link_hbm))
        ]

    list_copy = pltpu.make_async_copy(list_hbm, list_ref, local_sems.at[3])
    list_copy.start()
    for copy in local_copies():
        copy.start()

    field = lax.broadcasted_iota(jnp.int32, (8, size), 0)
    scale = jnp.where(field < 4, jnp.float32(length_scale), jnp.float32(width_scale))

    def prepare(tile, carry):
        row_ref[tile] = joined_ref[pl.ds(tile, 8, stride=rows_all), :] * scale
        return carry

    lax.fori_loop(0, rows_all, prepare, 0, unroll=8)
    row_ref[rows_all] = jnp.ones((8, size), jnp.float32)
    fill_vectors(joined_ref, 5 * rows_all, rows_all, vec_ref)

    atom = lax.broadcasted_iota(jnp.int32, (size, size), 0)
    partner_atom = lax.broadcasted_iota(jnp.int32, (size, size), 1)
    apart_ref[...] = jnp.where(atom == partner_atom, jnp.inf, 0.0).astype(jnp.float32)

    line = lax.broadcasted_iota(jnp.int32, (32, 5 * size), 0)
    chosen = lax.broadcasted_iota(jnp.int32, (32, 5 * size), 1) // size
    select = jnp.where(((line & 7) == chosen) & (line < 24), 1.0, 0.0).astype(jnp.bfloat16)

    def spread(tile, carry):
        params = row_ref[tile]
        stacked = jnp.concatenate(split_rows(params) + [jnp.zeros_like(params)], axis=0)
        spread_ref[tile] = lax.dot_general(
            stacked.astype(jnp.bfloat16), select, (((0,), (0,)), ((), ())), preferred_element_type=jnp.float32)
        sum_ref[tile] = jnp.zeros(sum_ref.shape[1:], jnp.float32)
        return carry

    lax.fori_loop(0, tiles, spread, 0, unroll=2)
    sum_ref[tiles] = jnp.zeros(sum_ref.shape[1:], jnp.float32)

    def multiply(ring_ref, base, entries, kind):
        blocks = [lambda place=place: ring_ref[base, place] for place in range(BUILD_PAIRS)]
        add_products(vec_ref, sum_ref, blocks, entries, kind)

    def out_copy(ring_ref, half, base, first):
        return pltpu.make_async_copy(
            ring_ref.at[base], store_ref.at[pl.ds(first, BUILD_PAIRS)], sems.at[half, base])

    def pair_block(ring_ref, base, slot, entry, own_pairs):
        own = jnp.minimum(own_of(entry), tiles - 1)
        partner = partner_of(entry)
        place, lanes = slot // 2, slice(slot % 2 * size, slot % 2 * size + size)
        shift_a = (((entry >> 8) & 3) - 1).astype(jnp.float32) * length_scale
        shift_b = (((entry >> 10) & 3) - 1).astype(jnp.float32) * length_scale
        shift_c = (((entry >> 12) & 3) - 1).astype(jnp.float32) * length_scale
        theirs = row_ref[partner]
        full = (16, size)
        their_a = jnp.broadcast_to(theirs[0:1] + shift_a, full)
        their_b = jnp.broadcast_to(theirs[1:2] + shift_b, full)
        their_c = jnp.broadcast_to(theirs[2:3] + shift_c, full)
        their_shield = jnp.broadcast_to(theirs[3:4], full)
        their_width = jnp.broadcast_to(theirs[4:5], full)
        for group in range(size // 16):
            rows = slice(16 * group, 16 * group + 16)

            def mine(c):
                return spread_ref[own, rows, c * size : (c + 1) * size]

            delta_a = their_a - mine(0)
            delta_b = their_b - mine(1)
            delta_c = their_c - mine(2)
            distance = delta_a * delta_a + delta_b * delta_b + delta_c * delta_c
            if own_pairs:
                distance = distance + apart_ref[rows, :]
            coulomb = lax.rsqrt(distance + mine(3) * their_shield)
            response = response_scale * jnp.exp2(distance / (mine(4) + their_width))
            ring_ref[base, place, rows, lanes] = coulomb.astype(jnp.bfloat16)
            ring_ref[base, place, size + 16 * group : size + 16 * group + 16, lanes] = response.astype(jnp.bfloat16)

    def entries_at(first):
        return [list_ref[first + slot] for slot in range(BUILD_SLOTS)]

    def turns(first, last, kind):
        def visit(turn, carry):
            base = lax.rem(turn, BUILD_RING)
            before = lax.rem(turn + BUILD_RING - 1, BUILD_RING)
            start = turn * TURN

            @pl.when(turn >= BUILD_RING)
            def _():
                out_copy(even_ref, 0, base, 0).wait()
                out_copy(odd_ref, 1, base, 0).wait()

            late = [
                jnp.where(turn > first, list_ref[jnp.maximum(start - BUILD_SLOTS + slot, 0)], nothing)
                for slot in range(BUILD_SLOTS)
            ]
            even, odd = entries_at(start), entries_at(start + BUILD_SLOTS)
            multiply(odd_ref, before, late, kind)
            for slot, entry in enumerate(even):
                pair_block(even_ref, base, slot, entry, kind == "own")
            multiply(even_ref, base, even, kind)
            for slot, entry in enumerate(odd):
                pair_block(odd_ref, base, slot, entry, kind == "own")
            out_copy(even_ref, 0, base, 2 * BUILD_PAIRS * turn).start()
            out_copy(odd_ref, 1, base, 2 * BUILD_PAIRS * turn + BUILD_PAIRS).start()
            return carry

        lax.fori_loop(first, last, visit, 0)

        @pl.when(last > first)
        def _():
            final = last - 1
            multiply(odd_ref, lax.rem(final, BUILD_RING), entries_at(final * TURN + BUILD_SLOTS), kind)

    nothing = packed(tiles, rows_all)
    assert tiles % TURN == 0
    own_turns = tiles // TURN
    list_copy.wait()
    halo_turns = list_ref[list_ref.shape[0] - 2]
    all_turns = list_ref[list_ref.shape[0] - 1]
    turns(0, jnp.minimum(halo_turns, own_turns), "own")
    turns(own_turns, halo_turns, "halo")
    turns(halo_turns, all_turns, "inner")
    for group in range(BUILD_RING):
        @pl.when(group < all_turns)
        def _():
            out_copy(even_ref, 0, group, 0).wait()
            out_copy(odd_ref, 1, group, 0).wait()

    for copy in local_copies():
        copy.wait()

    def finish(tile, carry):
        total = sum_ref[tile]
        one = pl.ds(tile, 1)
        diag_charge = local_ref[0, one, :] + total[12:13, 0:128] - SHIFT
        diag_potential = local_ref[1, one, :] + total[12:13, 128:256] - SHIFT
        linking = local_ref[2, one, :]
        diag_ref[0, one, :] = diag_charge
        diag_ref[1, one, :] = diag_potential
        diag_ref[2, one, :] = linking
        values = joined_ref[pl.ds(5 * rows_all + tile, 4, stride=rows_all), :]
        pair_charge, pair_potential = pair_parts(total)
        image_ref[pl.ds(tile, 4, stride=tiles), :] = image_rows(
            values, pair_charge, pair_potential, diag_charge, diag_potential, linking)
        return carry

    lax.fori_loop(0, tiles, finish, 0, unroll=4)


def apply_kernel(*refs):
    list_hbm, joined_ref, diag_hbm, store_ref = refs[:4]
    last = len(refs) > 12
    earlier_hbm = refs[4:6] if last else ()
    image_ref = refs[4 + len(earlier_hbm)]
    moment_ref = refs[7] if last else None
    vec_ref, sum_ref, ring_ref, diag_ref, list_ref = refs[8:13] if last else refs[5:10]
    earlier_refs = refs[13:15] if last else ()
    sems, local_sems = refs[-2:]

    tiles = diag_hbm.shape[1]
    rows_all = vec_ref.shape[0] - 1
    own_turns = tiles // TURN

    def in_copy(turn, first=0, places=TURN // 2):
        slot = lax.rem(turn, APPLY_RING)
        return pltpu.make_async_copy(
            store_ref.at[pl.ds(turn * (TURN // 2) + first, places)],
            ring_ref.at[slot, pl.ds(first, places)], sems.at[slot])

    def start_copies(turn):
        for first in range(0, TURN // 2, APPLY_COPY):
            in_copy(turn, first, APPLY_COPY).start()

    def local_copies():
        pairs = [(diag_hbm, diag_ref)] + list(zip(earlier_hbm, earlier_refs))
        return [
            pltpu.make_async_copy(source, target, local_sems.at[place])
            for place, (source, target) in enumerate(pairs)
        ]

    ahead = APPLY_RING - 1
    list_copy = pltpu.make_async_copy(list_hbm, list_ref, local_sems.at[len(earlier_hbm) + 1])
    list_copy.start()
    for turn in range(min(ahead, own_turns)):
        start_copies(jnp.int32(turn))
    for copy in local_copies():
        copy.start()

    fill_vectors(joined_ref, 0, rows_all, vec_ref)

    def clear(tile, carry):
        sum_ref[tile] = jnp.zeros(sum_ref.shape[1:], jnp.float32)
        return carry

    lax.fori_loop(0, tiles + 1, clear, 0, unroll=4)

    list_copy.wait()
    halo_turns = list_ref[list_ref.shape[0] - 2]
    all_turns = list_ref[list_ref.shape[0] - 1]
    for turn in range(own_turns, ahead):
        @pl.when(turn < all_turns)
        def _():
            start_copies(jnp.int32(turn))

    def visits(first, last, kind):
        def visit(turn, carry):
            slot = lax.rem(turn, APPLY_RING)

            @pl.when(turn + ahead < all_turns)
            def _():
                start_copies(turn + ahead)

            in_copy(turn).wait()
            entries = [list_ref[turn * TURN + place] for place in range(TURN)]
            blocks = [lambda place=place: ring_ref[slot, place] for place in range(TURN // 2)]
            add_products(vec_ref, sum_ref, blocks, entries, kind)
            return carry

        lax.fori_loop(first, last, visit, 0)

    visits(0, own_turns, "own")
    visits(own_turns, halo_turns, "halo")
    visits(halo_turns, all_turns, "inner")
    for copy in local_copies():
        copy.wait()

    def finish(tile, carry):
        total = sum_ref[tile]
        one = pl.ds(tile, 1)
        values = joined_ref[pl.ds(tile, 4, stride=rows_all), :]
        pair_charge, pair_potential = pair_parts(total)
        image_ref[pl.ds(tile, 4, stride=tiles), :] = image_rows(
            values, pair_charge, pair_potential, diag_ref[0, one, :], diag_ref[1, one, :], diag_ref[2, one, :])
        return carry

    lax.fori_loop(0, tiles, finish, 0, unroll=4)

    if last:
        lane = lax.broadcasted_iota(jnp.int32, (1, 128), 1)

        def rows_of(order, field):
            if order == 2:
                return joined_ref[field * rows_all : field * rows_all + tiles, :]
            ref = (earlier_refs[0], earlier_refs[1], None, image_ref)[order]
            return ref[field * tiles : (field + 1) * tiles, :]

        lines = []
        for system in range(2):
            line = jnp.zeros((1, 128), jnp.float32)
            for degree in range(2 * ITERS):
                left, right = degree // 2, degree - degree // 2
                product = rows_of(left, system) * rows_of(right, system)
                product = product + rows_of(left, 2 + system) * rows_of(right, 2 + system)
                line = jnp.where(lane == degree, jnp.sum(product, keepdims=True), line)
            lines.append(line)
        both = jnp.concatenate(lines, axis=0)
        moment_ref[...] = jnp.broadcast_to(both[None], moment_ref.shape)


def combine_kernel(moments_ref, zero_ref, one_ref, two_ref, three_ref, solution_ref, residual_ref):
    tiles = zero_ref.shape[0] // 4
    total = jnp.sum(moments_ref[...], axis=0)
    moments = [total[:, degree : degree + 1] for degree in range(2 * ITERS)]

    def times(poly):
        grown = [SHIFT * c for c in poly] + [jnp.zeros_like(poly[0])]
        return [c + p for c, p in zip(grown, [jnp.zeros_like(poly[0])] + poly)]

    def product(left, right):
        out = 0.0
        for i, a in enumerate(left):
            for j, c in enumerate(right):
                out = out + a * c * moments[i + j]
        return out

    def axpy(left, scale, right):
        length = max(len(left), len(right))
        zero = jnp.zeros_like(scale)
        left = left + [zero] * (length - len(left))
        right = right + [zero] * (length - len(right))
        return [a + scale * c for a, c in zip(left, right)]

    one = jnp.ones_like(moments[0])
    found = [jnp.zeros_like(one)]
    rest = [one]
    direction = [one]
    norm = moments[0]
    for iteration in range(ITERS):
        along = times(direction)
        step = norm / product(direction, along)
        found = axpy(found, step, direction)
        rest = axpy(rest, -step, along)
        if iteration + 1 < ITERS:
            norm_next = product(rest, rest)
            direction = axpy(rest, norm_next / norm, direction)
            norm = norm_next
    refs = (zero_ref, one_ref, two_ref, three_ref)
    for field in range(4):
        system = field % 2
        span = slice(field * tiles, field * tiles + tiles)
        for poly, out_ref in ((found, solution_ref), (rest, residual_ref)):
            value = 0.0
            for c, ref in zip(poly, refs):
                value = value + c[system : system + 1, :] * ref[span, :]
            out_ref[span, :] = value


VMEM = pltpu.MemorySpace.VMEM
SMEM = pltpu.MemorySpace.SMEM


def in_vmem():
    return pl.BlockSpec(memory_space=VMEM)


def in_hbm():
    return pl.BlockSpec(memory_space=pltpu.MemorySpace.HBM)


def pinned(array):
    return pltpu.with_memory_space_constraint(array, pltpu.MemorySpace.HBM)


def in_smem():
    return pl.BlockSpec(memory_space=SMEM)


def on_device(positions, shield, width, hardness, softness, coupling, pair_bits, right_side):
    extent = hardness.shape[:3]
    size = hardness.shape[3]
    tiles = extent[0] * extent[1] * extent[2]
    counts = {axis: lax.axis_size(axis) for axis in AXES}
    f32 = jnp.float32

    hard, soft, link = (a.reshape(tiles, size) for a in (hardness, softness, coupling))
    start = right_side.reshape(4, tiles, size)
    fields = jnp.concatenate(
        [positions.reshape(3, tiles, size), shield.reshape(1, tiles, size), width.reshape(1, tiles, size), start],
        axis=0)
    joined, boxes = extended(fields, extent)
    rows_all = joined.shape[1]
    halo, inner = candidate_pairs(boxes, extent, counts)
    entries = tiles + sum(-(-len(found) // 2) * 2 for found in halo + inner)
    entries = -(-(entries + 3 * TURN) // TURN) * TURN

    tables = [jnp.asarray(list_table(found, packed(tiles, rows_all))) for found in (halo, inner)]
    slots = pl.pallas_call(
        functools.partial(list_kernel, spare=rows_all),
        out_shape=jax.ShapeDtypeStruct((entries + 2,), jnp.int32),
        in_specs=[in_smem()] * 3,
        out_specs=in_smem(),
        scratch_shapes=[pltpu.SMEM((tiles,), jnp.int32)],
        name="pair_list",
    )(pair_bits, *tables)
    slots = pinned(slots)

    flat = (4 * tiles, size)
    start_flat = start.reshape(flat)
    store, diag, image = pl.pallas_call(
        build_kernel,
        out_shape=(
            jax.ShapeDtypeStruct((entries // 2, 2 * size, 2 * size), jnp.bfloat16),
            jax.ShapeDtypeStruct((3, tiles, size), f32),
            jax.ShapeDtypeStruct(flat, f32),
        ),
        in_specs=[in_hbm(), in_vmem()] + [in_hbm()] * 3,
        out_specs=(in_hbm(), in_vmem(), in_vmem()),
        scratch_shapes=[
            pltpu.VMEM((rows_all + 1, 8, size), f32),
            pltpu.VMEM((tiles, size, 5 * size), f32),
            pltpu.VMEM((rows_all + 1, 16, size), jnp.bfloat16),
            pltpu.VMEM((tiles + 1, 16, 2 * size), f32),
            pltpu.VMEM((BUILD_RING, BUILD_PAIRS, 2 * size, 2 * size), jnp.bfloat16),
            pltpu.VMEM((BUILD_RING, BUILD_PAIRS, 2 * size, 2 * size), jnp.bfloat16),
            pltpu.VMEM((3, tiles, size), f32),
            pltpu.SMEM((entries + 2,), jnp.int32),
            pltpu.VMEM((size, size), f32),
            pltpu.SemaphoreType.DMA((2, BUILD_RING)),
            pltpu.SemaphoreType.DMA((4,)),
        ],
        compiler_params=pltpu.CompilerParams(vmem_limit_bytes=40 * 2**20),
        name="build",
    )(slots, joined.reshape(-1, size), pinned(hard), pinned(soft), pinned(link))

    devices = counts["gx"] * counts["gy"] * counts["gz"]
    diag = pinned(diag)

    def operate(vector, earlier=()):
        spread, _ = extended(vector.reshape(4, tiles, size), extent)
        last = len(earlier) > 0
        more = len(earlier)
        image_shape = jax.ShapeDtypeStruct(flat, f32)
        moment_shape = jax.ShapeDtypeStruct((devices, 2, size), f32)
        return pl.pallas_call(
            apply_kernel,
            out_shape=(image_shape, moment_shape) if last else image_shape,
            in_specs=[in_hbm(), in_vmem()] + [in_hbm()] * (2 + more),
            out_specs=(in_vmem(), in_vmem()) if last else in_vmem(),
            scratch_shapes=[
                pltpu.VMEM((rows_all + 1, 16, size), jnp.bfloat16),
                pltpu.VMEM((tiles + 1, 16, 2 * size), f32),
                pltpu.VMEM((APPLY_RING, TURN // 2, 2 * size, 2 * size), jnp.bfloat16),
                pltpu.VMEM((3, tiles, size), f32),
                pltpu.SMEM((entries + 2,), jnp.int32),
            ] + [pltpu.VMEM(flat, f32)] * more + [
                pltpu.SemaphoreType.DMA((APPLY_RING,)),
                pltpu.SemaphoreType.DMA((2 + more,)),
            ],
            compiler_params=pltpu.CompilerParams(vmem_limit_bytes=40 * 2**20),
            name="apply_last" if last else "apply",
        )(slots, spread.reshape(-1, size), diag, store, *[pinned(v) for v in earlier])

    second = operate(image)
    third, moments = operate(second, (start_flat, image))
    vectors = (start_flat, image, second, third)
    gathered = lax.all_to_all(moments, AXES, 0, 0)
    solution, residual = pl.pallas_call(
        combine_kernel,
        out_shape=(jax.ShapeDtypeStruct(flat, f32), jax.ShapeDtypeStruct(flat, f32)),
        in_specs=[in_vmem()] * 5,
        out_specs=(in_vmem(), in_vmem()),
        name="combine",
    )(gathered, *vectors)
    return (solution.reshape(right_side.shape), residual.reshape(right_side.shape))


def solution(mesh):
    return jax.shard_map(
        on_device,
        mesh=mesh,
        in_specs=(
            P(None, "gx", "gy", "gz", None),
            P("gx", "gy", "gz", None),
            P("gx", "gy", "gz", None),
            P("gx", "gy", "gz", None),
            P("gx", "gy", "gz", None),
            P("gx", "gy", "gz", None),
            P("gx", "gy", "gz"),
            P(None, "gx", "gy", "gz", None),
        ),
        out_specs=(P(None, "gx", "gy", "gz", None), P(None, "gx", "gy", "gz", None)),
        check_vma=False,
    )
```

time: 136 us -> 114 us (0.84); the launches traced: 134 us -> 114 us
  Pallas kernels: 61.6 us -> 48.9 us
  local copies, waits for them, and re-layouts: 10.2 us -> 1.8 us
  waiting for transfers between devices: 25.4 us -> 23.2 us
  starting transfers between devices: 21.2 us -> 22.9 us
  blocking collectives: 12 us -> 13.5 us
    pallas_call x5 -> x4, Pallas kernels: 59.7 us -> 47 us  [the longest x2 21.5 us: operate(): pl.pallas_call(apply_kernel, out_shape=(image_shape, moment_shape) if las...]
    ppermute x6, starting transfers between devices: 9.3 us -> 2.38 us  [extended(): high = lax.ppermute(first, axis, backward)]
    ppermute x3, starting transfers between devices: 2.37 us -> 7.62 us  [extended(): got = lax.ppermute(sent, axis, [(0, 1), (1, 0)])]
    unnamed x28 -> x16, local copies, waits for them, and re-layouts: 5.72 us -> 0.66 us
    ppermute x3, waiting for transfers between devices: 9.27 us -> 5.09 us  [extended(): got = lax.ppermute(sent, axis, [(0, 1), (1, 0)])]
    ppermute x6, starting transfers between devices: 9.53 us -> 12.9 us  [extended(): low = lax.ppermute(last, axis, forward)]
    all_to_all x1, blocking collectives: 12 us -> 13.5 us  [on_device(): gathered = lax.all_to_all(moments, AXES, 0, 0)]
  transfers between devices with their start and end apart: 15 -> 15, of which waited for: 12 -> 13; matrix products, arithmetic and copies ran while one was open for 2% -> 2% of each run, Pallas kernels for 2% -> 4%
where the time goes in v2:
time: 114 us
  Pallas kernels  48.9 us (43%)
  waiting for transfers between devices  23.2 us (20%)
  starting transfers between devices  22.9 us (20%)
  blocking collectives  13.5 us (12%)
  other arithmetic  2.83 us (2%)
  local copies, waits for them, and re-layouts  1.8 us (2%)
    pallas_call x2, Pallas kernels, operate(): pl.pallas_call(apply_kernel, out_shape=(image_shape, moment_shape) if las...  21.5 us
    pallas_call x1, Pallas kernels, on_device(): pl.pallas_call(build_kernel, out_shape=(jax.ShapeDtypeStruct((entries //...  21.5 us
    all_to_all x1, blocking collectives, on_device(): gathered = lax.all_to_all(moments, AXES, 0, 0)  13.5 us
    ppermute x6, starting transfers between devices, extended(): low = lax.ppermute(last, axis, forward)  12.9 us
    ppermute x6, waiting for transfers between devices, extended(): low = lax.ppermute(last, axis, forward)  11 us
    ppermute x3, starting transfers between devices, extended(): got = lax.ppermute(sent, axis, [(0, 1), (1, 0)])  7.62 us
    ppermute x6, waiting for transfers between devices, extended(): high = lax.ppermute(first, axis, backward)  7.09 us
    ppermute x3, waiting for transfers between devices, extended(): got = lax.ppermute(sent, axis, [(0, 1), (1, 0)])  5.09 us
  transfers between devices with their start and end apart: 15, of which 13 were waited for; matrix products, arithmetic and copies ran while one was open for 2% of the time, Pallas kernels for 4%

profile of v2, /device:TPU:0, one launch (start us, length us, event | category | flops | bytes accessed | tf_op | source)
XLA Modules:
  0.0 114.1 jit_solution(16646237470008492221)
XLA Ops:
  0.6 0.9 pad_maximum_fusion.1
  1.5 3.1 %collective-permute-start = (f32[9,16,128]{2,1,0:T(8,128)S(1)}, f32[9,16,128]{2,1,0:T(8,128)S(1)}, u32[]{:S(2)}, u32[]{:S(2)}) collective-permute-start(f32[9,16,128]{2,1,0:T(8,128)S(1)} %fusion), channel_id=1, source_target_pairs={{0,4},{4,0},{1,5},{5,1},{2,6},{6,2},{3,7},{7,3},{8,12},{12,8},{9,1... | collective-permute-start | bytes 221192 | tf_op jit(solution)/shard_map/ppermute | solution.py:78
  4.6 1.0 pad_maximum_fusion.8
  5.6 1.3 %collective-permute-done = f32[9,16,128]{2,1,0:T(8,128)S(1)} collective-permute-done((f32[9,16,128]{2,1,0:T(8,128)S(1)}, f32[9,16,128]{2,1,0:T(8,128)S(1)}, u32[]{:S(2)}, u32[]{:S(2)}) %collective-permute-start) | collective-permute-done | bytes 73760 | tf_op jit(solution)/shard_map/ppermute | solution.py:78
  7.0 2.1 %collective-permute-start.1 = (f32[9,24,128]{2,1,0:T(8,128)S(1)}, f32[9,24,128]{2,1,0:T(8,128)S(1)}, u32[]{:S(2)}, u32[]{:S(2)}) collective-permute-start(f32[9,24,128]{2,1,0:T(8,128)S(1)} %pad_maximum_fusion.2), channel_id=1, source_target_pairs={{0,8},{8,16},{16,24},{24,0},{1,9},{9,17},{17,25},{25,1},{2,10},{10... | collective-permute-start | bytes 331784 | tf_op jit(solution)/shard_map/ppermute | solution.py:83
  9.1 2.1 %collective-permute-start.2 = (f32[9,24,128]{2,1,0:T(8,128)S(1)}, f32[9,24,128]{2,1,0:T(8,128)S(1)}, u32[]{:S(2)}, u32[]{:S(2)}) collective-permute-start(f32[9,24,128]{2,1,0:T(8,128)S(1)} %pad_maximum_fusion.3), channel_id=1, source_target_pairs={{8,0},{16,8},{24,16},{0,24},{9,1},{17,9},{25,17},{1,25},{10,2},{18... | collective-permute-start | bytes 331784 | tf_op jit(solution)/shard_map/ppermute | solution.py:84
  11.2 3.4 %collective-permute-done.1 = f32[9,24,128]{2,1,0:T(8,128)S(1)} collective-permute-done((f32[9,24,128]{2,1,0:T(8,128)S(1)}, f32[9,24,128]{2,1,0:T(8,128)S(1)}, u32[]{:S(2)}, u32[]{:S(2)}) %collective-permute-start.1) | collective-permute-done | bytes 110624 | tf_op jit(solution)/shard_map/ppermute | solution.py:83
  14.7 0.4 collective-permute-done.2
  15.2 0.1 concatenate.62
  15.2 0.1 collective-permute-start.4
  15.3 0.1 concatenate.61
  15.4 0.5 collective-permute-start.3
  15.9 0.9 pad_maximum_fusion
  16.8 4.0 %pair_list.1.list_hbm.refs_0_ = s32[778]{0:T(1024)} custom-call(s32[2,2,8]{2,1,0:T(2,128)} %bits_ref.1, s32[608]{0:T(1024)} %constant.12.clone.halo_ref, s32[320]{0:T(512)} %constant.13.clone.inner_ref), custom_call_target="tpu_custom_call" | custom-call | tf_op jit(solution)/shard_map/pair_list/pallas_call | solution.py:612
  20.8 0.0 collective-permute-done.4
  20.8 0.0 collective-permute-done.3
  20.9 0.2 concatenate.63
  21.0 21.5 %build.1 = (bf16[388,256,256]{2,1,0:T(8,128)(2,1)}, f32[3,32,128]{2,1,0:T(8,128)S(1)}, f32[128,128]{1,0:T(8,128)S(1)}) custom-call(s32[778]{0:T(1024)} %pair_list.1.list_hbm.refs_0_, f32[1080,128]{1,0:T(8,128)S(1)} %bitcast.142, f32[32,128]{1,0:T(8,128)} %bitcast.199, f32[32,128]{1,0:T(8,128)} %bitcast.200, f32[32,128]{1,0:T(8,128)} %bitcast.201), custom_call_target="tpu_custom_call" | custom-call | tf_op jit(solution)/shard_map/build/pallas_call | solution.py:624
  42.5 0.0 copy-start.2
  42.5 0.6 copy-done.2
  43.1 0.0 copy-start
  43.2 2.1 %collective-permute-start.5 = (f32[4,16,128]{2,1,0:T(8,128)S(1)}, f32[4,16,128]{2,1,0:T(8,128)S(1)}, u32[]{:S(2)}, u32[]{:S(2)}) collective-permute-start(f32[4,16,128]{2,1,0:T(8,128)S(1)} %fusion.2), channel_id=1, source_target_pairs={{0,4},{4,0},{1,5},{5,1},{2,6},{6,2},{3,7},{7,3},{8,12},{12,8},{9,1... | collective-permute-start | bytes 98312 | tf_op jit(solution)/shard_map/ppermute | solution.py:78
  45.3 1.8 %collective-permute-done.5 = f32[4,16,128]{2,1,0:T(8,128)S(1)} collective-permute-done((f32[4,16,128]{2,1,0:T(8,128)S(1)}, f32[4,16,128]{2,1,0:T(8,128)S(1)}, u32[]{:S(2)}, u32[]{:S(2)}) %collective-permute-start.5) | collective-permute-done | bytes 32800 | tf_op jit(solution)/shard_map/ppermute | solution.py:78
  47.2 5.0 %collective-permute-start.6 = (f32[4,24,128]{2,0,1:T(4,128)S(1)}, f32[4,24,128]{2,0,1:T(4,128)S(1)}, u32[]{:S(2)}, u32[]{:S(2)}) collective-permute-start(f32[4,24,128]{2,0,1:T(4,128)S(1)} %pad_maximum_fusion.4), channel_id=1, source_target_pairs={{0,8},{8,16},{16,24},{24,0},{1,9},{9,17},{17,25},{25,1},{2,10},{10... | collective-permute-start | bytes 147464 | tf_op jit(solution)/shard_map/ppermute | solution.py:83
  52.3 0.1 collective-permute-start.7
  52.4 1.6 %collective-permute-done.6 = f32[4,24,128]{2,0,1:T(4,128)S(1)} collective-permute-done((f32[4,24,128]{2,0,1:T(4,128)S(1)}, f32[4,24,128]{2,0,1:T(4,128)S(1)}, u32[]{:S(2)}, u32[]{:S(2)}) %collective-permute-start.6) | collective-permute-done | bytes 49184 | tf_op jit(solution)/shard_map/ppermute | solution.py:83
  54.0 2.7 %collective-permute-done.7 = f32[4,24,128]{2,0,1:T(4,128)S(1)} collective-permute-done((f32[4,24,128]{2,0,1:T(4,128)S(1)}, f32[4,24,128]{2,0,1:T(4,128)S(1)}, u32[]{:S(2)}, u32[]{:S(2)}) %collective-permute-start.7) | collective-permute-done | bytes 49184 | tf_op jit(solution)/shard_map/ppermute | solution.py:84
  56.8 0.1 concatenate.67
  56.9 0.1 collective-permute-start.9
  56.9 0.1 concatenate.66
  57.0 0.5 collective-permute-start.8
  57.5 1.0 collective-permute-done.9
  58.5 2.0 %collective-permute-done.8 = f32[4,12,128]{2,1,0:T(8,128)S(1)} collective-permute-done((f32[4,12,128]{2,1,0:T(8,128)S(1)}, f32[4,12,128]{2,1,0:T(8,128)S(1)}, u32[]{:S(2)}, u32[]{:S(2)}) %collective-permute-start.8) | collective-permute-done | bytes 24608 | tf_op jit(solution)/shard_map/ppermute | solution.py:83
  60.5 0.1 concatenate.68
  60.7 10.7 %apply.1.two_ref = f32[128,128]{1,0:T(8,128)S(1)} custom-call(s32[778]{0:T(1024)} %pair_list.1.list_hbm.refs_0_, f32[480,128]{1,0:T(8,128)S(1)} %bitcast.152, f32[3,32,128]{2,1,0:T(8,128)} %copy-done.2, bf16[388,256,256]{2,1,0:T(8,128)(2,1)} %get-tuple-element.11.refs_3_), custom_call_target="tpu_custom_call" | custom-call | tf_op jit(solution)/shard_map/apply/pallas_call | solution.py:659
  71.4 0.0 copy-start.1
  71.4 2.4 %collective-permute-start.10 = (f32[4,16,128]{2,1,0:T(8,128)S(1)}, f32[4,16,128]{2,1,0:T(8,128)S(1)}, u32[]{:S(2)}, u32[]{:S(2)}) collective-permute-start(f32[4,16,128]{2,1,0:T(8,128)S(1)} %fusion.1), channel_id=1, source_target_pairs={{0,4},{4,0},{1,5},{5,1},{2,6},{6,2},{3,7},{7,3},{8,12},{12,8},{9,1... | collective-permute-start | bytes 98312 | tf_op jit(solution)/shard_map/ppermute | solution.py:78
  73.9 1.9 %collective-permute-done.10 = f32[4,16,128]{2,1,0:T(8,128)S(1)} collective-permute-done((f32[4,16,128]{2,1,0:T(8,128)S(1)}, f32[4,16,128]{2,1,0:T(8,128)S(1)}, u32[]{:S(2)}, u32[]{:S(2)}) %collective-permute-start.10) | collective-permute-done | bytes 32800 | tf_op jit(solution)/shard_map/ppermute | solution.py:78
  75.9 4.1 %collective-permute-start.11 = (f32[4,24,128]{2,0,1:T(4,128)S(1)}, f32[4,24,128]{2,0,1:T(4,128)S(1)}, u32[]{:S(2)}, u32[]{:S(2)}) collective-permute-start(f32[4,24,128]{2,0,1:T(4,128)S(1)} %pad_maximum_fusion.6), channel_id=1, source_target_pairs={{0,8},{8,16},{16,24},{24,0},{1,9},{9,17},{17,25},{25,1},{2,10},{10... | collective-permute-start | bytes 147464 | tf_op jit(solution)/shard_map/ppermute | solution.py:83
  80.0 0.1 collective-permute-start.12
  80.1 2.0 %collective-permute-done.11 = f32[4,24,128]{2,0,1:T(4,128)S(1)} collective-permute-done((f32[4,24,128]{2,0,1:T(4,128)S(1)}, f32[4,24,128]{2,0,1:T(4,128)S(1)}, u32[]{:S(2)}, u32[]{:S(2)}) %collective-permute-start.11) | collective-permute-done | bytes 49184 | tf_op jit(solution)/shard_map/ppermute | solution.py:83
  82.2 2.0 %collective-permute-done.12 = f32[4,24,128]{2,0,1:T(4,128)S(1)} collective-permute-done((f32[4,24,128]{2,0,1:T(4,128)S(1)}, f32[4,24,128]{2,0,1:T(4,128)S(1)}, u32[]{:S(2)}, u32[]{:S(2)}) %collective-permute-start.12) | collective-permute-done | bytes 49184 | tf_op jit(solution)/shard_map/ppermute | solution.py:84
  84.2 0.1 concatenate.72
  84.3 0.1 collective-permute-start.14
  84.3 0.1 concatenate.71
  84.4 0.5 collective-permute-start.13
  84.9 1.0 collective-permute-done.14
  85.9 1.8 %collective-permute-done.13 = f32[4,12,128]{2,1,0:T(8,128)S(1)} collective-permute-done((f32[4,12,128]{2,1,0:T(8,128)S(1)}, f32[4,12,128]{2,1,0:T(8,128)S(1)}, u32[]{:S(2)}, u32[]{:S(2)}) %collective-permute-start.13) | collective-permute-done | bytes 24608 | tf_op jit(solution)/shard_map/ppermute | solution.py:83
  87.8 0.1 concatenate.73
  87.9 0.0 copy-done
  87.9 10.8 %apply_last.1 = (f32[128,128]{1,0:T(8,128)S(1)}, f32[32,2,128]{2,1,0:T(2,128)S(1)}) custom-call(s32[778]{0:T(1024)} %pair_list.1.list_hbm.refs_0_, f32[480,128]{1,0:T(8,128)S(1)} %bitcast.151, f32[3,32,128]{2,1,0:T(8,128)} %copy-done.2, bf16[388,256,256]{2,1,0:T(8,128)(2,1)} %get-tuple-element.11.refs_3_, f32[128,128]{1,0:T(8,128)} %bitcast.154, ...), custom_call_target="tpu_custom_call" | custom-call | tf_op jit(solution)/shard_map/apply_last/pallas_call | solution.py:659
  98.8 0.0 copy-start.3
  98.8 13.5 %all_to_all.5.moments_ref = f32[32,2,128]{2,1,0:T(2,128)} all-to-all(f32[32,2,128]{2,1,0:T(2,128)S(1)} %get-tuple-element.12), channel_id=1, replica_groups=mesh['gx'=4,'gy'=2,'gz'=4] {'gx','gy','gz'}, dimensions={0} | all-to-all | bytes 65536 | tf_op jit(solution)/shard_map/all_to_all | solution.py:681
  112.3 0.0 copy-done.1
  112.3 0.0 copy-done.3
  112.3 1.8 %combine.1 = (f32[128,128]{1,0:T(8,128)}, f32[128,128]{1,0:T(8,128)}) custom-call(f32[32,2,128]{2,1,0:T(2,128)} %all_to_all.5.moments_ref, f32[128,128]{1,0:T(8,128)} %bitcast.155, f32[128,128]{1,0:T(8,128)} %copy-done, f32[128,128]{1,0:T(8,128)} %copy-done.1, f32[128,128]{1,0:T(8,128)} %copy-done.3), custom_call_target="tpu_custom_call" | custom-call | tf_op jit(solution)/shard_map/combine/pallas_call | solution.py:682
  (65 shorter events, 0.5 us)
Async XLA Ops:
  1.5 5.4 %collective-permute-start = (f32[9,16,128]{2,1,0:T(8,128)S(1)}, f32[9,16,128]{2,1,0:T(8,128)S(1)}, u32[]{:S(2)}, u32[]{:S(2)}) collective-permute-start(f32[9,16,128]{2,1,0:T(8,128)S(1)} %fusion), channel_id=1, source_target_pairs={{0,4},{4,0},{1,5},{5,1},{2,6},{6,2},{3,7},{7,3},{8,12},{12,8},{9,1... | collective-permute-start | bytes 221192 | tf_op jit(solution)/shard_map/ppermute | solution.py:78
  7.0 7.7 %collective-permute-start.1 = (f32[9,24,128]{2,1,0:T(8,128)S(1)}, f32[9,24,128]{2,1,0:T(8,128)S(1)}, u32[]{:S(2)}, u32[]{:S(2)}) collective-permute-start(f32[9,24,128]{2,1,0:T(8,128)S(1)} %pad_maximum_fusion.2), channel_id=1, source_target_pairs={{0,8},{8,16},{16,24},{24,0},{1,9},{9,17},{17,25},{25,1},{2,10},{10... | collective-permute-start | bytes 331784 | tf_op jit(solution)/shard_map/ppermute | solution.py:83
  9.1 6.0 %collective-permute-start.2 = (f32[9,24,128]{2,1,0:T(8,128)S(1)}, f32[9,24,128]{2,1,0:T(8,128)S(1)}, u32[]{:S(2)}, u32[]{:S(2)}) collective-permute-start(f32[9,24,128]{2,1,0:T(8,128)S(1)} %pad_maximum_fusion.3), channel_id=1, source_target_pairs={{8,0},{16,8},{24,16},{0,24},{9,1},{17,9},{25,17},{1,25},{10,2},{18... | collective-permute-start | bytes 331784 | tf_op jit(solution)/shard_map/ppermute | solution.py:84
  15.2 5.6 %collective-permute-start.4 = (f32[9,12,128]{2,1,0:T(8,128)S(1)}, f32[9,12,128]{2,1,0:T(8,128)S(1)}, u32[]{:S(2)}, u32[]{:S(2)}) collective-permute-start(f32[9,12,128]{2,1,0:T(8,128)S(1)} %concatenate.62), channel_id=1, source_target_pairs={{1,0},{2,1},{3,2},{0,3},{5,4},{6,5},{7,6},{4,7},{9,8},{10,9},{11,1... | collective-permute-start | bytes 165896 | tf_op jit(solution)/shard_map/ppermute | solution.py:84
  15.4 5.5 %collective-permute-start.3 = (f32[9,12,128]{2,1,0:T(8,128)S(1)}, f32[9,12,128]{2,1,0:T(8,128)S(1)}, u32[]{:S(2)}, u32[]{:S(2)}) collective-permute-start(f32[9,12,128]{2,1,0:T(8,128)S(1)} %concatenate.61), channel_id=1, source_target_pairs={{0,1},{1,2},{2,3},{3,0},{4,5},{5,6},{6,7},{7,4},{8,9},{9,10},{10,1... | collective-permute-start | bytes 165896 | tf_op jit(solution)/shard_map/ppermute | solution.py:83
  42.5 0.6 copy-start.2
  43.1 44.8 %copy-start = (f32[128,128]{1,0:T(8,128)}, f32[128,128]{1,0:T(8,128)S(1)}, u32[]{:S(2)}) copy-start(f32[128,128]{1,0:T(8,128)S(1)} %get-tuple-element.9.refs_5_.one_ref) | copy-start | bytes 196612
  43.2 4.0 %collective-permute-start.5 = (f32[4,16,128]{2,1,0:T(8,128)S(1)}, f32[4,16,128]{2,1,0:T(8,128)S(1)}, u32[]{:S(2)}, u32[]{:S(2)}) collective-permute-start(f32[4,16,128]{2,1,0:T(8,128)S(1)} %fusion.2), channel_id=1, source_target_pairs={{0,4},{4,0},{1,5},{5,1},{2,6},{6,2},{3,7},{7,3},{8,12},{12,8},{9,1... | collective-permute-start | bytes 98312 | tf_op jit(solution)/shard_map/ppermute | solution.py:78
  47.2 6.8 %collective-permute-start.6 = (f32[4,24,128]{2,0,1:T(4,128)S(1)}, f32[4,24,128]{2,0,1:T(4,128)S(1)}, u32[]{:S(2)}, u32[]{:S(2)}) collective-permute-start(f32[4,24,128]{2,0,1:T(4,128)S(1)} %pad_maximum_fusion.4), channel_id=1, source_target_pairs={{0,8},{8,16},{16,24},{24,0},{1,9},{9,17},{17,25},{25,1},{2,10},{10... | collective-permute-start | bytes 147464 | tf_op jit(solution)/shard_map/ppermute | solution.py:83
  52.3 4.5 %collective-permute-start.7 = (f32[4,24,128]{2,0,1:T(4,128)S(1)}, f32[4,24,128]{2,0,1:T(4,128)S(1)}, u32[]{:S(2)}, u32[]{:S(2)}) collective-permute-start(f32[4,24,128]{2,0,1:T(4,128)S(1)} %pad_maximum_fusion.5), channel_id=1, source_target_pairs={{8,0},{16,8},{24,16},{0,24},{9,1},{17,9},{25,17},{1,25},{10,2},{18... | collective-permute-start | bytes 147464 | tf_op jit(solution)/shard_map/ppermute | solution.py:84
  56.9 1.7 %collective-permute-start.9 = (f32[4,12,128]{2,1,0:T(8,128)S(1)}, f32[4,12,128]{2,1,0:T(8,128)S(1)}, u32[]{:S(2)}, u32[]{:S(2)}) collective-permute-start(f32[4,12,128]{2,1,0:T(8,128)S(1)} %concatenate.67), channel_id=1, source_target_pairs={{1,0},{2,1},{3,2},{0,3},{5,4},{6,5},{7,6},{4,7},{9,8},{10,9},{11,1... | collective-permute-start | bytes 73736 | tf_op jit(solution)/shard_map/ppermute | solution.py:84
  57.0 3.6 %collective-permute-start.8 = (f32[4,12,128]{2,1,0:T(8,128)S(1)}, f32[4,12,128]{2,1,0:T(8,128)S(1)}, u32[]{:S(2)}, u32[]{:S(2)}) collective-permute-start(f32[4,12,128]{2,1,0:T(8,128)S(1)} %concatenate.66), channel_id=1, source_target_pairs={{0,1},{1,2},{2,3},{3,0},{4,5},{5,6},{6,7},{7,4},{8,9},{9,10},{10,1... | collective-permute-start | bytes 73736 | tf_op jit(solution)/shard_map/ppermute | solution.py:83
  71.4 40.9 %copy-start.1 = (f32[128,128]{1,0:T(8,128)}, f32[128,128]{1,0:T(8,128)S(1)}, u32[]{:S(2)}) copy-start(f32[128,128]{1,0:T(8,128)S(1)} %apply.1.two_ref) | copy-start | bytes 196612
  71.4 4.4 %collective-permute-start.10 = (f32[4,16,128]{2,1,0:T(8,128)S(1)}, f32[4,16,128]{2,1,0:T(8,128)S(1)}, u32[]{:S(2)}, u32[]{:S(2)}) collective-permute-start(f32[4,16,128]{2,1,0:T(8,128)S(1)} %fusion.1), channel_id=1, source_target_pairs={{0,4},{4,0},{1,5},{5,1},{2,6},{6,2},{3,7},{7,3},{8,12},{12,8},{9,1... | collective-permute-start | bytes 98312 | tf_op jit(solution)/shard_map/ppermute | solution.py:78
  75.9 6.2 %collective-permute-start.11 = (f32[4,24,128]{2,0,1:T(4,128)S(1)}, f32[4,24,128]{2,0,1:T(4,128)S(1)}, u32[]{:S(2)}, u32[]{:S(2)}) collective-permute-start(f32[4,24,128]{2,0,1:T(4,128)S(1)} %pad_maximum_fusion.6), channel_id=1, source_target_pairs={{0,8},{8,16},{16,24},{24,0},{1,9},{9,17},{17,25},{25,1},{2,10},{10... | collective-permute-start | bytes 147464 | tf_op jit(solution)/shard_map/ppermute | solution.py:83
  80.0 4.1 %collective-permute-start.12 = (f32[4,24,128]{2,0,1:T(4,128)S(1)}, f32[4,24,128]{2,0,1:T(4,128)S(1)}, u32[]{:S(2)}, u32[]{:S(2)}) collective-permute-start(f32[4,24,128]{2,0,1:T(4,128)S(1)} %pad_maximum_fusion.7), channel_id=1, source_target_pairs={{8,0},{16,8},{24,16},{0,24},{9,1},{17,9},{25,17},{1,25},{10,2},{18... | collective-permute-start | bytes 147464 | tf_op jit(solution)/shard_map/ppermute | solution.py:84
  84.3 1.7 %collective-permute-start.14 = (f32[4,12,128]{2,1,0:T(8,128)S(1)}, f32[4,12,128]{2,1,0:T(8,128)S(1)}, u32[]{:S(2)}, u32[]{:S(2)}) collective-permute-start(f32[4,12,128]{2,1,0:T(8,128)S(1)} %concatenate.72), channel_id=1, source_target_pairs={{1,0},{2,1},{3,2},{0,3},{5,4},{6,5},{7,6},{4,7},{9,8},{10,9},{11,1... | collective-permute-start | bytes 73736 | tf_op jit(solution)/shard_map/ppermute | solution.py:84
  84.4 3.4 %collective-permute-start.13 = (f32[4,12,128]{2,1,0:T(8,128)S(1)}, f32[4,12,128]{2,1,0:T(8,128)S(1)}, u32[]{:S(2)}, u32[]{:S(2)}) collective-permute-start(f32[4,12,128]{2,1,0:T(8,128)S(1)} %concatenate.71), channel_id=1, source_target_pairs={{0,1},{1,2},{2,3},{3,0},{4,5},{5,6},{6,7},{7,4},{8,9},{9,10},{10,1... | collective-permute-start | bytes 73736 | tf_op jit(solution)/shard_map/ppermute | solution.py:83
  98.8 13.5 %copy-start.3 = (f32[128,128]{1,0:T(8,128)}, f32[128,128]{1,0:T(8,128)S(1)}, u32[]{:S(2)}) copy-start(f32[128,128]{1,0:T(8,128)S(1)} %get-tuple-element.13.three_ref) | copy-start | bytes 196612

commit v3 on v2

--- a/solution.py
+++ b/solution.py
@@ -27,7 +27,8 @@
 BUILD_PAIRS = BUILD_SLOTS // 2
 BUILD_RING = 8
 APPLY_COPY = 1
-APPLY_RING = 10
+APPLY_RING = 12
+APPLY_MERGE = 3
 
 
 class Piece:
@@ -298,7 +299,7 @@
         sum_ref[tile] = jnp.zeros(sum_ref.shape[1:], jnp.float32)
         return carry
 
-    lax.fori_loop(0, tiles, spread, 0, unroll=2)
+    lax.fori_loop(0, tiles, spread, 0, unroll=8)
     sum_ref[tiles] = jnp.zeros(sum_ref.shape[1:], jnp.float32)
 
     def multiply(ring_ref, base, entries, kind):
@@ -443,7 +444,7 @@
             for place, (source, target) in enumerate(pairs)
         ]
 
-    ahead = APPLY_RING - 1
+    ahead = APPLY_RING - APPLY_MERGE
     list_copy = pltpu.make_async_copy(list_hbm, list_ref, local_sems.at[len(earlier_hbm) + 1])
     list_copy.start()
     for turn in range(min(ahead, own_turns)):
@@ -468,22 +469,35 @@
             start_copies(jnp.int32(turn))
 
     def visits(first, last, kind):
-        def visit(turn, carry):
-            slot = lax.rem(turn, APPLY_RING)
-
-            @pl.when(turn + ahead < all_turns)
-            def _():
-                start_copies(turn + ahead)
-
-            in_copy(turn).wait()
-            entries = [list_ref[turn * TURN + place] for place in range(TURN)]
-            blocks = [lambda place=place: ring_ref[slot, place] for place in range(TURN // 2)]
+        def several(turn, merged):
+            for step in range(merged):
+                @pl.when(turn + step + ahead < all_turns)
+                def _():
+                    start_copies(turn + step + ahead)
+
+            for step in range(merged):
+                in_copy(turn + step).wait()
+            entries = [list_ref[turn * TURN + place] for place in range(merged * TURN)]
+            blocks = [
+                lambda slot=lax.rem(turn + step, APPLY_RING), place=place: ring_ref[slot, place]
+                for step in range(merged)
+                for place in range(TURN // 2)
+            ]
             add_products(vec_ref, sum_ref, blocks, entries, kind)
+
+        def visit_many(group, carry):
+            several(first + group * APPLY_MERGE, APPLY_MERGE)
             return carry
 
-        lax.fori_loop(first, last, visit, 0)
-
-    visits(0, own_turns, "own")
+        def visit_one(turn, carry):
+            several(turn, 1)
+            return carry
+
+        groups = (last - first) // APPLY_MERGE
+        lax.fori_loop(0, groups, visit_many, 0)
+        lax.fori_loop(first + groups * APPLY_MERGE, last, visit_one, 0)
+
+    visits(0, jnp.minimum(halo_turns, own_turns), "own")
     visits(own_turns, halo_turns, "halo")
     visits(halo_turns, all_turns, "inner")
     for copy in local_copies():

time: 114 us -> 107 us (0.939)
  Pallas kernels: 48.9 us -> 43 us
  starting transfers between devices: 22.9 us -> 21.2 us
  waiting for transfers between devices: 23.2 us -> 24.5 us
    pallas_call x2, Pallas kernels: 21.5 us -> 17.9 us  [operate(): pl.pallas_call(apply_kernel, out_shape=(image_shape, moment_shape) if las...]
    ppermute x6, starting transfers between devices: 12.9 us -> 10.1 us  [extended(): low = lax.ppermute(last, axis, forward)]
    ppermute x6, waiting for transfers between devices: 11 us -> 13.6 us  [extended(): low = lax.ppermute(last, axis, forward)]
    pallas_call x1, Pallas kernels: 21.5 us -> 19.3 us  [on_device(): pl.pallas_call(build_kernel, out_shape=(jax.ShapeDtypeStruct((entries //...]
    ppermute x6, starting transfers between devices: 2.38 us -> 4.44 us  [extended(): high = lax.ppermute(first, axis, backward)]
    ppermute x6, waiting for transfers between devices: 7.09 us -> 5.06 us  [extended(): high = lax.ppermute(first, axis, backward)]
where the time goes in v3:
time: 107 us
  Pallas kernels  43 us (40%)
  waiting for transfers between devices  24.5 us (23%)
  starting transfers between devices  21.2 us (20%)
  blocking collectives  12.8 us (12%)
  other arithmetic  2.83 us (3%)
  local copies, waits for them, and re-layouts  1.8 us (2%)
  between operations  1.11 us (1%)
    pallas_call x1, Pallas kernels, on_device(): pl.pallas_call(build_kernel, out_shape=(jax.ShapeDtypeStruct((entries //...  19.3 us
    pallas_call x2, Pallas kernels, operate(): pl.pallas_call(apply_kernel, out_shape=(image_shape, moment_shape) if las...  17.9 us
    ppermute x6, waiting for transfers between devices, extended(): low = lax.ppermute(last, axis, forward)  13.6 us
    all_to_all x1, blocking collectives, on_device(): gathered = lax.all_to_all(moments, AXES, 0, 0)  12.8 us
    ppermute x6, starting transfers between devices, extended(): low = lax.ppermute(last, axis, forward)  10.1 us
    ppermute x3, starting transfers between devices, extended(): got = lax.ppermute(sent, axis, [(0, 1), (1, 0)])  6.69 us
    ppermute x3, waiting for transfers between devices, extended(): got = lax.ppermute(sent, axis, [(0, 1), (1, 0)])  5.88 us
    ppermute x6, waiting for transfers between devices, extended(): high = lax.ppermute(first, axis, backward)  5.06 us
  transfers between devices with their start and end apart: 15, of which 13 were waited for; matrix products, arithmetic and copies ran while one was open for 2% of the time, Pallas kernels for 4%

profile of v3, /device:TPU:0, one launch (start us, length us, event | category | flops | bytes accessed | tf_op | source)
XLA Modules:
  0.0 107.2 jit_solution(1816484072432776238)
XLA Ops:
  0.6 0.9 pad_maximum_fusion.1
  1.5 3.1 %collective-permute-start = (f32[9,16,128]{2,1,0:T(8,128)S(1)}, f32[9,16,128]{2,1,0:T(8,128)S(1)}, u32[]{:S(2)}, u32[]{:S(2)}) collective-permute-start(f32[9,16,128]{2,1,0:T(8,128)S(1)} %fusion), channel_id=1, source_target_pairs={{0,4},{4,0},{1,5},{5,1},{2,6},{6,2},{3,7},{7,3},{8,12},{12,8},{9,1... | collective-permute-start | bytes 221192 | tf_op jit(solution)/shard_map/ppermute | solution.py:79
  4.6 1.0 pad_maximum_fusion.8
  5.6 1.3 %collective-permute-done = f32[9,16,128]{2,1,0:T(8,128)S(1)} collective-permute-done((f32[9,16,128]{2,1,0:T(8,128)S(1)}, f32[9,16,128]{2,1,0:T(8,128)S(1)}, u32[]{:S(2)}, u32[]{:S(2)}) %collective-permute-start) | collective-permute-done | bytes 73760 | tf_op jit(solution)/shard_map/ppermute | solution.py:79
  7.0 2.1 %collective-permute-start.1 = (f32[9,24,128]{2,1,0:T(8,128)S(1)}, f32[9,24,128]{2,1,0:T(8,128)S(1)}, u32[]{:S(2)}, u32[]{:S(2)}) collective-permute-start(f32[9,24,128]{2,1,0:T(8,128)S(1)} %pad_maximum_fusion.2), channel_id=1, source_target_pairs={{0,8},{8,16},{16,24},{24,0},{1,9},{9,17},{17,25},{25,1},{2,10},{10... | collective-permute-start | bytes 331784 | tf_op jit(solution)/shard_map/ppermute | solution.py:84
  9.1 2.1 %collective-permute-start.2 = (f32[9,24,128]{2,1,0:T(8,128)S(1)}, f32[9,24,128]{2,1,0:T(8,128)S(1)}, u32[]{:S(2)}, u32[]{:S(2)}) collective-permute-start(f32[9,24,128]{2,1,0:T(8,128)S(1)} %pad_maximum_fusion.3), channel_id=1, source_target_pairs={{8,0},{16,8},{24,16},{0,24},{9,1},{17,9},{25,17},{1,25},{10,2},{18... | collective-permute-start | bytes 331784 | tf_op jit(solution)/shard_map/ppermute | solution.py:85
  11.2 3.4 %collective-permute-done.1 = f32[9,24,128]{2,1,0:T(8,128)S(1)} collective-permute-done((f32[9,24,128]{2,1,0:T(8,128)S(1)}, f32[9,24,128]{2,1,0:T(8,128)S(1)}, u32[]{:S(2)}, u32[]{:S(2)}) %collective-permute-start.1) | collective-permute-done | bytes 110624 | tf_op jit(solution)/shard_map/ppermute | solution.py:84
  14.7 0.4 collective-permute-done.2
  15.2 0.1 concatenate.62
  15.2 0.1 collective-permute-start.4
  15.3 0.1 concatenate.61
  15.4 0.5 collective-permute-start.3
  15.9 0.9 pad_maximum_fusion
  16.8 4.0 %pair_list.1.list_hbm.refs_0_ = s32[778]{0:T(1024)} custom-call(s32[2,2,8]{2,1,0:T(2,128)} %bits_ref.1, s32[608]{0:T(1024)} %constant.12.clone.halo_ref, s32[320]{0:T(512)} %constant.13.clone.inner_ref), custom_call_target="tpu_custom_call" | custom-call | tf_op jit(solution)/shard_map/pair_list/pallas_call | solution.py:626
  20.8 0.0 collective-permute-done.4
  20.8 0.0 collective-permute-done.3
  20.9 0.2 concatenate.63
  21.0 19.3 %build.1 = (bf16[388,256,256]{2,1,0:T(8,128)(2,1)}, f32[3,32,128]{2,1,0:T(8,128)S(1)}, f32[128,128]{1,0:T(8,128)S(1)}) custom-call(s32[778]{0:T(1024)} %pair_list.1.list_hbm.refs_0_, f32[1080,128]{1,0:T(8,128)S(1)} %bitcast.142, f32[32,128]{1,0:T(8,128)} %bitcast.199, f32[32,128]{1,0:T(8,128)} %bitcast.200, f32[32,128]{1,0:T(8,128)} %bitcast.201), custom_call_target="tpu_custom_call" | custom-call | tf_op jit(solution)/shard_map/build/pallas_call | solution.py:638
  40.3 0.0 copy-start.2
  40.3 0.6 copy-done.2
  40.9 0.0 copy-start
  40.9 2.1 %collective-permute-start.5 = (f32[4,16,128]{2,1,0:T(8,128)S(1)}, f32[4,16,128]{2,1,0:T(8,128)S(1)}, u32[]{:S(2)}, u32[]{:S(2)}) collective-permute-start(f32[4,16,128]{2,1,0:T(8,128)S(1)} %fusion.2), channel_id=1, source_target_pairs={{0,4},{4,0},{1,5},{5,1},{2,6},{6,2},{3,7},{7,3},{8,12},{12,8},{9,1... | collective-permute-start | bytes 98312 | tf_op jit(solution)/shard_map/ppermute | solution.py:79
  43.1 1.8 %collective-permute-done.5 = f32[4,16,128]{2,1,0:T(8,128)S(1)} collective-permute-done((f32[4,16,128]{2,1,0:T(8,128)S(1)}, f32[4,16,128]{2,1,0:T(8,128)S(1)}, u32[]{:S(2)}, u32[]{:S(2)}) %collective-permute-start.5) | collective-permute-done | bytes 32800 | tf_op jit(solution)/shard_map/ppermute | solution.py:79
  45.0 4.5 %collective-permute-start.6 = (f32[4,24,128]{2,0,1:T(4,128)S(1)}, f32[4,24,128]{2,0,1:T(4,128)S(1)}, u32[]{:S(2)}, u32[]{:S(2)}) collective-permute-start(f32[4,24,128]{2,0,1:T(4,128)S(1)} %pad_maximum_fusion.4), channel_id=1, source_target_pairs={{0,8},{8,16},{16,24},{24,0},{1,9},{9,17},{17,25},{25,1},{2,10},{10... | collective-permute-start | bytes 147464 | tf_op jit(solution)/shard_map/ppermute | solution.py:84
  49.6 0.1 collective-permute-start.7
  49.7 2.0 %collective-permute-done.6 = f32[4,24,128]{2,0,1:T(4,128)S(1)} collective-permute-done((f32[4,24,128]{2,0,1:T(4,128)S(1)}, f32[4,24,128]{2,0,1:T(4,128)S(1)}, u32[]{:S(2)}, u32[]{:S(2)}) %collective-permute-start.6) | collective-permute-done | bytes 49184 | tf_op jit(solution)/shard_map/ppermute | solution.py:84
  51.7 2.0 %collective-permute-done.7 = f32[4,24,128]{2,0,1:T(4,128)S(1)} collective-permute-done((f32[4,24,128]{2,0,1:T(4,128)S(1)}, f32[4,24,128]{2,0,1:T(4,128)S(1)}, u32[]{:S(2)}, u32[]{:S(2)}) %collective-permute-start.7) | collective-permute-done | bytes 49184 | tf_op jit(solution)/shard_map/ppermute | solution.py:85
  53.8 0.1 concatenate.67
  53.9 0.4 collective-permute-start.9
  54.2 0.1 concatenate.66
  54.3 0.2 collective-permute-start.8
  54.5 1.3 %collective-permute-done.9 = f32[4,12,128]{2,1,0:T(8,128)S(1)} collective-permute-done((f32[4,12,128]{2,1,0:T(8,128)S(1)}, f32[4,12,128]{2,1,0:T(8,128)S(1)}, u32[]{:S(2)}, u32[]{:S(2)}) %collective-permute-start.9) | collective-permute-done | bytes 24608 | tf_op jit(solution)/shard_map/ppermute | solution.py:85
  55.8 3.6 %collective-permute-done.8 = f32[4,12,128]{2,1,0:T(8,128)S(1)} collective-permute-done((f32[4,12,128]{2,1,0:T(8,128)S(1)}, f32[4,12,128]{2,1,0:T(8,128)S(1)}, u32[]{:S(2)}, u32[]{:S(2)}) %collective-permute-start.8) | collective-permute-done | bytes 24608 | tf_op jit(solution)/shard_map/ppermute | solution.py:84
  59.4 0.1 concatenate.68
  59.6 8.8 %apply.1.two_ref = f32[128,128]{1,0:T(8,128)S(1)} custom-call(s32[778]{0:T(1024)} %pair_list.1.list_hbm.refs_0_, f32[480,128]{1,0:T(8,128)S(1)} %bitcast.152, f32[3,32,128]{2,1,0:T(8,128)} %copy-done.2, bf16[388,256,256]{2,1,0:T(8,128)(2,1)} %get-tuple-element.11.refs_3_), custom_call_target="tpu_custom_call" | custom-call | tf_op jit(solution)/shard_map/apply/pallas_call | solution.py:673
  68.4 0.0 copy-start.1
  68.4 1.5 %collective-permute-start.10 = (f32[4,16,128]{2,1,0:T(8,128)S(1)}, f32[4,16,128]{2,1,0:T(8,128)S(1)}, u32[]{:S(2)}, u32[]{:S(2)}) collective-permute-start(f32[4,16,128]{2,1,0:T(8,128)S(1)} %fusion.1), channel_id=1, source_target_pairs={{0,4},{4,0},{1,5},{5,1},{2,6},{6,2},{3,7},{7,3},{8,12},{12,8},{9,1... | collective-permute-start | bytes 98312 | tf_op jit(solution)/shard_map/ppermute | solution.py:79
  70.0 2.7 %collective-permute-done.10 = f32[4,16,128]{2,1,0:T(8,128)S(1)} collective-permute-done((f32[4,16,128]{2,1,0:T(8,128)S(1)}, f32[4,16,128]{2,1,0:T(8,128)S(1)}, u32[]{:S(2)}, u32[]{:S(2)}) %collective-permute-start.10) | collective-permute-done | bytes 32800 | tf_op jit(solution)/shard_map/ppermute | solution.py:79
  72.8 2.1 %collective-permute-start.11 = (f32[4,24,128]{2,0,1:T(4,128)S(1)}, f32[4,24,128]{2,0,1:T(4,128)S(1)}, u32[]{:S(2)}, u32[]{:S(2)}) collective-permute-start(f32[4,24,128]{2,0,1:T(4,128)S(1)} %pad_maximum_fusion.6), channel_id=1, source_target_pairs={{0,8},{8,16},{16,24},{24,0},{1,9},{9,17},{17,25},{25,1},{2,10},{10... | collective-permute-start | bytes 147464 | tf_op jit(solution)/shard_map/ppermute | solution.py:84
  74.9 1.8 %collective-permute-start.12 = (f32[4,24,128]{2,0,1:T(4,128)S(1)}, f32[4,24,128]{2,0,1:T(4,128)S(1)}, u32[]{:S(2)}, u32[]{:S(2)}) collective-permute-start(f32[4,24,128]{2,0,1:T(4,128)S(1)} %pad_maximum_fusion.7), channel_id=1, source_target_pairs={{8,0},{16,8},{24,16},{0,24},{9,1},{17,9},{25,17},{1,25},{10,2},{18... | collective-permute-start | bytes 147464 | tf_op jit(solution)/shard_map/ppermute | solution.py:85
  76.7 2.3 %collective-permute-done.11 = f32[4,24,128]{2,0,1:T(4,128)S(1)} collective-permute-done((f32[4,24,128]{2,0,1:T(4,128)S(1)}, f32[4,24,128]{2,0,1:T(4,128)S(1)}, u32[]{:S(2)}, u32[]{:S(2)}) %collective-permute-start.11) | collective-permute-done | bytes 49184 | tf_op jit(solution)/shard_map/ppermute | solution.py:84
  79.1 0.4 collective-permute-done.12
  79.5 0.1 concatenate.72
  79.5 0.1 collective-permute-start.14
  79.6 0.1 concatenate.71
  79.6 0.5 collective-permute-start.13
  80.2 1.0 collective-permute-done.14
  81.2 2.2 %collective-permute-done.13 = f32[4,12,128]{2,1,0:T(8,128)S(1)} collective-permute-done((f32[4,12,128]{2,1,0:T(8,128)S(1)}, f32[4,12,128]{2,1,0:T(8,128)S(1)}, u32[]{:S(2)}, u32[]{:S(2)}) %collective-permute-start.13) | collective-permute-done | bytes 24608 | tf_op jit(solution)/shard_map/ppermute | solution.py:84
  83.4 0.1 concatenate.73
  83.6 0.0 copy-done
  83.6 9.0 %apply_last.1 = (f32[128,128]{1,0:T(8,128)S(1)}, f32[32,2,128]{2,1,0:T(2,128)S(1)}) custom-call(s32[778]{0:T(1024)} %pair_list.1.list_hbm.refs_0_, f32[480,128]{1,0:T(8,128)S(1)} %bitcast.151, f32[3,32,128]{2,1,0:T(8,128)} %copy-done.2, bf16[388,256,256]{2,1,0:T(8,128)(2,1)} %get-tuple-element.11.refs_3_, f32[128,128]{1,0:T(8,128)} %bitcast.154, ...), custom_call_target="tpu_custom_call" | custom-call | tf_op jit(solution)/shard_map/apply_last/pallas_call | solution.py:673
  92.6 0.0 copy-start.3
  92.6 12.8 %all_to_all.5.moments_ref = f32[32,2,128]{2,1,0:T(2,128)} all-to-all(f32[32,2,128]{2,1,0:T(2,128)S(1)} %get-tuple-element.12), channel_id=1, replica_groups=mesh['gx'=4,'gy'=2,'gz'=4] {'gx','gy','gz'}, dimensions={0} | all-to-all | bytes 65536 | tf_op jit(solution)/shard_map/all_to_all | solution.py:695
  105.4 0.0 copy-done.1
  105.4 0.0 copy-done.3
  105.4 1.8 %combine.1 = (f32[128,128]{1,0:T(8,128)}, f32[128,128]{1,0:T(8,128)}) custom-call(f32[32,2,128]{2,1,0:T(2,128)} %all_to_all.5.moments_ref, f32[128,128]{1,0:T(8,128)} %bitcast.155, f32[128,128]{1,0:T(8,128)} %copy-done, f32[128,128]{1,0:T(8,128)} %copy-done.1, f32[128,128]{1,0:T(8,128)} %copy-done.3), custom_call_target="tpu_custom_call" | custom-call | tf_op jit(solution)/shard_map/combine/pallas_call | solution.py:696
  (65 shorter events, 0.5 us)
Async XLA Ops:
  1.5 5.4 %collective-permute-start = (f32[9,16,128]{2,1,0:T(8,128)S(1)}, f32[9,16,128]{2,1,0:T(8,128)S(1)}, u32[]{:S(2)}, u32[]{:S(2)}) collective-permute-start(f32[9,16,128]{2,1,0:T(8,128)S(1)} %fusion), channel_id=1, source_target_pairs={{0,4},{4,0},{1,5},{5,1},{2,6},{6,2},{3,7},{7,3},{8,12},{12,8},{9,1... | collective-permute-start | bytes 221192 | tf_op jit(solution)/shard_map/ppermute | solution.py:79
  7.0 7.7 %collective-permute-start.1 = (f32[9,24,128]{2,1,0:T(8,128)S(1)}, f32[9,24,128]{2,1,0:T(8,128)S(1)}, u32[]{:S(2)}, u32[]{:S(2)}) collective-permute-start(f32[9,24,128]{2,1,0:T(8,128)S(1)} %pad_maximum_fusion.2), channel_id=1, source_target_pairs={{0,8},{8,16},{16,24},{24,0},{1,9},{9,17},{17,25},{25,1},{2,10},{10... | collective-permute-start | bytes 331784 | tf_op jit(solution)/shard_map/ppermute | solution.py:84
  9.1 6.0 %collective-permute-start.2 = (f32[9,24,128]{2,1,0:T(8,128)S(1)}, f32[9,24,128]{2,1,0:T(8,128)S(1)}, u32[]{:S(2)}, u32[]{:S(2)}) collective-permute-start(f32[9,24,128]{2,1,0:T(8,128)S(1)} %pad_maximum_fusion.3), channel_id=1, source_target_pairs={{8,0},{16,8},{24,16},{0,24},{9,1},{17,9},{25,17},{1,25},{10,2},{18... | collective-permute-start | bytes 331784 | tf_op jit(solution)/shard_map/ppermute | solution.py:85
  15.2 5.6 %collective-permute-start.4 = (f32[9,12,128]{2,1,0:T(8,128)S(1)}, f32[9,12,128]{2,1,0:T(8,128)S(1)}, u32[]{:S(2)}, u32[]{:S(2)}) collective-permute-start(f32[9,12,128]{2,1,0:T(8,128)S(1)} %concatenate.62), channel_id=1, source_target_pairs={{1,0},{2,1},{3,2},{0,3},{5,4},{6,5},{7,6},{4,7},{9,8},{10,9},{11,1... | collective-permute-start | bytes 165896 | tf_op jit(solution)/shard_map/ppermute | solution.py:85
  15.4 5.5 %collective-permute-start.3 = (f32[9,12,128]{2,1,0:T(8,128)S(1)}, f32[9,12,128]{2,1,0:T(8,128)S(1)}, u32[]{:S(2)}, u32[]{:S(2)}) collective-permute-start(f32[9,12,128]{2,1,0:T(8,128)S(1)} %concatenate.61), channel_id=1, source_target_pairs={{0,1},{1,2},{2,3},{3,0},{4,5},{5,6},{6,7},{7,4},{8,9},{9,10},{10,1... | collective-permute-start | bytes 165896 | tf_op jit(solution)/shard_map/ppermute | solution.py:84
  40.3 0.6 copy-start.2
  40.9 42.6 %copy-start = (f32[128,128]{1,0:T(8,128)}, f32[128,128]{1,0:T(8,128)S(1)}, u32[]{:S(2)}) copy-start(f32[128,128]{1,0:T(8,128)S(1)} %get-tuple-element.9.refs_5_.one_ref) | copy-start | bytes 196612
  40.9 4.0 %collective-permute-start.5 = (f32[4,16,128]{2,1,0:T(8,128)S(1)}, f32[4,16,128]{2,1,0:T(8,128)S(1)}, u32[]{:S(2)}, u32[]{:S(2)}) collective-permute-start(f32[4,16,128]{2,1,0:T(8,128)S(1)} %fusion.2), channel_id=1, source_target_pairs={{0,4},{4,0},{1,5},{5,1},{2,6},{6,2},{3,7},{7,3},{8,12},{12,8},{9,1... | collective-permute-start | bytes 98312 | tf_op jit(solution)/shard_map/ppermute | solution.py:79
  45.0 6.7 %collective-permute-start.6 = (f32[4,24,128]{2,0,1:T(4,128)S(1)}, f32[4,24,128]{2,0,1:T(4,128)S(1)}, u32[]{:S(2)}, u32[]{:S(2)}) collective-permute-start(f32[4,24,128]{2,0,1:T(4,128)S(1)} %pad_maximum_fusion.4), channel_id=1, source_target_pairs={{0,8},{8,16},{16,24},{24,0},{1,9},{9,17},{17,25},{25,1},{2,10},{10... | collective-permute-start | bytes 147464 | tf_op jit(solution)/shard_map/ppermute | solution.py:84
  49.6 4.2 %collective-permute-start.7 = (f32[4,24,128]{2,0,1:T(4,128)S(1)}, f32[4,24,128]{2,0,1:T(4,128)S(1)}, u32[]{:S(2)}, u32[]{:S(2)}) collective-permute-start(f32[4,24,128]{2,0,1:T(4,128)S(1)} %pad_maximum_fusion.5), channel_id=1, source_target_pairs={{8,0},{16,8},{24,16},{0,24},{9,1},{17,9},{25,17},{1,25},{10,2},{18... | collective-permute-start | bytes 147464 | tf_op jit(solution)/shard_map/ppermute | solution.py:85
  53.9 2.0 %collective-permute-start.9 = (f32[4,12,128]{2,1,0:T(8,128)S(1)}, f32[4,12,128]{2,1,0:T(8,128)S(1)}, u32[]{:S(2)}, u32[]{:S(2)}) collective-permute-start(f32[4,12,128]{2,1,0:T(8,128)S(1)} %concatenate.67), channel_id=1, source_target_pairs={{1,0},{2,1},{3,2},{0,3},{5,4},{6,5},{7,6},{4,7},{9,8},{10,9},{11,1... | collective-permute-start | bytes 73736 | tf_op jit(solution)/shard_map/ppermute | solution.py:85
  54.3 5.1 %collective-permute-start.8 = (f32[4,12,128]{2,1,0:T(8,128)S(1)}, f32[4,12,128]{2,1,0:T(8,128)S(1)}, u32[]{:S(2)}, u32[]{:S(2)}) collective-permute-start(f32[4,12,128]{2,1,0:T(8,128)S(1)} %concatenate.66), channel_id=1, source_target_pairs={{0,1},{1,2},{2,3},{3,0},{4,5},{5,6},{6,7},{7,4},{8,9},{9,10},{10,1... | collective-permute-start | bytes 73736 | tf_op jit(solution)/shard_map/ppermute | solution.py:84
  68.4 37.0 %copy-start.1 = (f32[128,128]{1,0:T(8,128)}, f32[128,128]{1,0:T(8,128)S(1)}, u32[]{:S(2)}) copy-start(f32[128,128]{1,0:T(8,128)S(1)} %apply.1.two_ref) | copy-start | bytes 196612
  68.4 4.3 %collective-permute-start.10 = (f32[4,16,128]{2,1,0:T(8,128)S(1)}, f32[4,16,128]{2,1,0:T(8,128)S(1)}, u32[]{:S(2)}, u32[]{:S(2)}) collective-permute-start(f32[4,16,128]{2,1,0:T(8,128)S(1)} %fusion.1), channel_id=1, source_target_pairs={{0,4},{4,0},{1,5},{5,1},{2,6},{6,2},{3,7},{7,3},{8,12},{12,8},{9,1... | collective-permute-start | bytes 98312 | tf_op jit(solution)/shard_map/ppermute | solution.py:79
  72.8 6.2 %collective-permute-start.11 = (f32[4,24,128]{2,0,1:T(4,128)S(1)}, f32[4,24,128]{2,0,1:T(4,128)S(1)}, u32[]{:S(2)}, u32[]{:S(2)}) collective-permute-start(f32[4,24,128]{2,0,1:T(4,128)S(1)} %pad_maximum_fusion.6), channel_id=1, source_target_pairs={{0,8},{8,16},{16,24},{24,0},{1,9},{9,17},{17,25},{25,1},{2,10},{10... | collective-permute-start | bytes 147464 | tf_op jit(solution)/shard_map/ppermute | solution.py:84
  74.9 4.5 %collective-permute-start.12 = (f32[4,24,128]{2,0,1:T(4,128)S(1)}, f32[4,24,128]{2,0,1:T(4,128)S(1)}, u32[]{:S(2)}, u32[]{:S(2)}) collective-permute-start(f32[4,24,128]{2,0,1:T(4,128)S(1)} %pad_maximum_fusion.7), channel_id=1, source_target_pairs={{8,0},{16,8},{24,16},{0,24},{9,1},{17,9},{25,17},{1,25},{10,2},{18... | collective-permute-start | bytes 147464 | tf_op jit(solution)/shard_map/ppermute | solution.py:85
  79.5 1.7 %collective-permute-start.14 = (f32[4,12,128]{2,1,0:T(8,128)S(1)}, f32[4,12,128]{2,1,0:T(8,128)S(1)}, u32[]{:S(2)}, u32[]{:S(2)}) collective-permute-start(f32[4,12,128]{2,1,0:T(8,128)S(1)} %concatenate.72), channel_id=1, source_target_pairs={{1,0},{2,1},{3,2},{0,3},{5,4},{6,5},{7,6},{4,7},{9,8},{10,9},{11,1... | collective-permute-start | bytes 73736 | tf_op jit(solution)/shard_map/ppermute | solution.py:85
  79.6 3.8 %collective-permute-start.13 = (f32[4,12,128]{2,1,0:T(8,128)S(1)}, f32[4,12,128]{2,1,0:T(8,128)S(1)}, u32[]{:S(2)}, u32[]{:S(2)}) collective-permute-start(f32[4,12,128]{2,1,0:T(8,128)S(1)} %concatenate.71), channel_id=1, source_target_pairs={{0,1},{1,2},{2,3},{3,0},{4,5},{5,6},{6,7},{7,4},{8,9},{9,10},{10,1... | collective-permute-start | bytes 73736 | tf_op jit(solution)/shard_map/ppermute | solution.py:84
  92.6 12.8 %copy-start.3 = (f32[128,128]{1,0:T(8,128)}, f32[128,128]{1,0:T(8,128)S(1)}, u32[]{:S(2)}) copy-start(f32[128,128]{1,0:T(8,128)S(1)} %get-tuple-element.13.three_ref) | copy-start | bytes 196612

commit v4 on v3

--- a/solution.py
+++ b/solution.py
@@ -410,7 +410,7 @@
             values, pair_charge, pair_potential, diag_charge, diag_potential, linking)
         return carry
 
-    lax.fori_loop(0, tiles, finish, 0, unroll=4)
+    lax.fori_loop(0, tiles, finish, 0, unroll=8)
 
 
 def apply_kernel(*refs):
@@ -512,7 +512,7 @@
             values, pair_charge, pair_potential, diag_ref[0, one, :], diag_ref[1, one, :], diag_ref[2, one, :])
         return carry
 
-    lax.fori_loop(0, tiles, finish, 0, unroll=4)
+    lax.fori_loop(0, tiles, finish, 0, unroll=8)
 
     if last:
         lane = lax.broadcasted_iota(jnp.int32, (1, 128), 1)
@@ -616,6 +616,7 @@
     fields = jnp.concatenate(
         [positions.reshape(3, tiles, size), shield.reshape(1, tiles, size), width.reshape(1, tiles, size), start],
         axis=0)
+    fields = lax.optimization_barrier(fields)
     joined, boxes = extended(fields, extent)
     rows_all = joined.shape[1]
     halo, inner = candidate_pairs(boxes, extent, counts)

time: 107 us -> 106 us (level)
  starting transfers between devices: 21.2 us -> 23.1 us
  other arithmetic: 2.83 us -> 0.97 us
    ppermute x3, starting transfers between devices: 6.69 us -> 8.59 us  [extended(): got = lax.ppermute(sent, axis, [(0, 1), (1, 0)])]
    ppermute x6, waiting for transfers between devices: 13.6 us -> 12 us  [extended(): low = lax.ppermute(last, axis, forward)]
    ppermute x6, starting transfers between devices: 10.1 us -> 11.4 us  [extended(): low = lax.ppermute(last, axis, forward)]
    ppermute x6, starting transfers between devices: 4.44 us -> 3.13 us  [extended(): high = lax.ppermute(first, axis, backward)]
  transfers between devices with their start and end apart: 15 -> 15, of which waited for: 13 -> 13; matrix products, arithmetic and copies ran while one was open for 2% -> 0% of each run, Pallas kernels for 4% -> 4%
where the time goes in v4:
time: 106 us; the launch traced here: 105 us
  Pallas kernels  42.3 us (40%)
  waiting for transfers between devices  24.1 us (23%)
  starting transfers between devices  23.1 us (22%)
  blocking collectives  11.9 us (11%)
  local copies, waits for them, and re-layouts  1.82 us (2%)
  between operations  1.12 us (1%)
    pallas_call x1, Pallas kernels, on_device(): pl.pallas_call(build_kernel, out_shape=(jax.ShapeDtypeStruct((entries //...  18.8 us
    pallas_call x2, Pallas kernels, operate(): pl.pallas_call(apply_kernel, out_shape=(image_shape, moment_shape) if las...  17.6 us
    ppermute x6, waiting for transfers between devices, extended(): low = lax.ppermute(last, axis, forward)  12 us
    all_to_all x1, blocking collectives, on_device(): gathered = lax.all_to_all(moments, AXES, 0, 0)  11.9 us
    ppermute x6, starting transfers between devices, extended(): low = lax.ppermute(last, axis, forward)  11.4 us
    ppermute x3, starting transfers between devices, extended(): got = lax.ppermute(sent, axis, [(0, 1), (1, 0)])  8.59 us
    ppermute x3, waiting for transfers between devices, extended(): got = lax.ppermute(sent, axis, [(0, 1), (1, 0)])  6.09 us
    ppermute x6, waiting for transfers between devices, extended(): high = lax.ppermute(first, axis, backward)  5.92 us
  transfers between devices with their start and end apart: 15, of which 13 were waited for; matrix products, arithmetic and copies ran while one was open for 0% of the time, Pallas kernels for 4%

profile of v4, /device:TPU:0, one launch (start us, length us, event | category | flops | bytes accessed | tf_op | source)
XLA Modules:
  0.0 105.3 jit_solution(18169244543434709338)
XLA Ops:
  0.6 0.9 pad_maximum_fusion
  1.5 3.1 %collective-permute-start = (f32[9,16,128]{2,1,0:T(8,128)S(1)}, f32[9,16,128]{2,1,0:T(8,128)S(1)}, u32[]{:S(2)}, u32[]{:S(2)}) collective-permute-start(f32[9,16,128]{2,1,0:T(8,128)S(1)} %fusion.1), channel_id=1, source_target_pairs={{0,4},{4,0},{1,5},{5,1},{2,6},{6,2},{3,7},{7,3},{8,12},{12,8},{9,1... | collective-permute-start | bytes 221192 | tf_op jit(solution)/shard_map/ppermute | solution.py:79
  4.6 2.3 %collective-permute-done = f32[9,16,128]{2,1,0:T(8,128)S(1)} collective-permute-done((f32[9,16,128]{2,1,0:T(8,128)S(1)}, f32[9,16,128]{2,1,0:T(8,128)S(1)}, u32[]{:S(2)}, u32[]{:S(2)}) %collective-permute-start) | collective-permute-done | bytes 73760 | tf_op jit(solution)/shard_map/ppermute | solution.py:79
  7.0 2.1 %collective-permute-start.1 = (f32[9,24,128]{2,1,0:T(8,128)S(1)}, f32[9,24,128]{2,1,0:T(8,128)S(1)}, u32[]{:S(2)}, u32[]{:S(2)}) collective-permute-start(f32[9,24,128]{2,1,0:T(8,128)S(1)} %pad_maximum_fusion.1), channel_id=1, source_target_pairs={{0,8},{8,16},{16,24},{24,0},{1,9},{9,17},{17,25},{25,1},{2,10},{10... | collective-permute-start | bytes 331784 | tf_op jit(solution)/shard_map/ppermute | solution.py:84
  9.1 2.1 %collective-permute-start.2 = (f32[9,24,128]{2,1,0:T(8,128)S(1)}, f32[9,24,128]{2,1,0:T(8,128)S(1)}, u32[]{:S(2)}, u32[]{:S(2)}) collective-permute-start(f32[9,24,128]{2,1,0:T(8,128)S(1)} %pad_maximum_fusion.2), channel_id=1, source_target_pairs={{8,0},{16,8},{24,16},{0,24},{9,1},{17,9},{25,17},{1,25},{10,2},{18... | collective-permute-start | bytes 331784 | tf_op jit(solution)/shard_map/ppermute | solution.py:85
  11.2 3.4 %collective-permute-done.1 = f32[9,24,128]{2,1,0:T(8,128)S(1)} collective-permute-done((f32[9,24,128]{2,1,0:T(8,128)S(1)}, f32[9,24,128]{2,1,0:T(8,128)S(1)}, u32[]{:S(2)}, u32[]{:S(2)}) %collective-permute-start.1) | collective-permute-done | bytes 110624 | tf_op jit(solution)/shard_map/ppermute | solution.py:84
  14.7 0.4 collective-permute-done.2
  15.2 0.1 concatenate.52
  15.2 0.1 collective-permute-start.4
  15.3 0.1 concatenate.51
  15.4 0.5 collective-permute-start.3
  15.9 4.0 %pair_list.1.list_hbm.refs_0_ = s32[778]{0:T(1024)} custom-call(s32[2,2,8]{2,1,0:T(2,128)} %bits_ref.1, s32[608]{0:T(1024)} %constant.12.clone.halo_ref, s32[320]{0:T(512)} %constant.13.clone.inner_ref), custom_call_target="tpu_custom_call" | custom-call | tf_op jit(solution)/shard_map/pair_list/pallas_call | solution.py:627
  19.9 0.0 collective-permute-done.4
  20.0 0.0 collective-permute-done.3
  20.0 0.2 concatenate.53
  20.2 18.8 %build.1 = (bf16[388,256,256]{2,1,0:T(8,128)(2,1)}, f32[3,32,128]{2,1,0:T(8,128)S(1)}, f32[128,128]{1,0:T(8,128)S(1)}) custom-call(s32[778]{0:T(1024)} %pair_list.1.list_hbm.refs_0_, f32[1080,128]{1,0:T(8,128)S(1)} %bitcast.159, f32[32,128]{1,0:T(8,128)} %bitcast.215, f32[32,128]{1,0:T(8,128)} %bitcast.216, f32[32,128]{1,0:T(8,128)} %bitcast.217), custom_call_target="tpu_custom_call" | custom-call | tf_op jit(solution)/shard_map/build/pallas_call | solution.py:639
  39.0 0.0 copy-start.2
  39.0 0.6 copy-done.2
  39.6 0.0 copy-start
  39.6 3.1 %collective-permute-start.5 = (f32[4,16,128]{2,1,0:T(8,128)S(1)}, f32[4,16,128]{2,1,0:T(8,128)S(1)}, u32[]{:S(2)}, u32[]{:S(2)}) collective-permute-start(f32[4,16,128]{2,1,0:T(8,128)S(1)} %fusion.3), channel_id=1, source_target_pairs={{0,4},{4,0},{1,5},{5,1},{2,6},{6,2},{3,7},{7,3},{8,12},{12,8},{9,1... | collective-permute-start | bytes 98312 | tf_op jit(solution)/shard_map/ppermute | solution.py:79
  42.7 1.8 %collective-permute-done.5 = f32[4,16,128]{2,1,0:T(8,128)S(1)} collective-permute-done((f32[4,16,128]{2,1,0:T(8,128)S(1)}, f32[4,16,128]{2,1,0:T(8,128)S(1)}, u32[]{:S(2)}, u32[]{:S(2)}) %collective-permute-start.5) | collective-permute-done | bytes 32800 | tf_op jit(solution)/shard_map/ppermute | solution.py:79
  44.6 4.6 %collective-permute-start.6 = (f32[4,24,128]{2,0,1:T(4,128)S(1)}, f32[4,24,128]{2,0,1:T(4,128)S(1)}, u32[]{:S(2)}, u32[]{:S(2)}) collective-permute-start(f32[4,24,128]{2,0,1:T(4,128)S(1)} %pad_maximum_fusion.3), channel_id=1, source_target_pairs={{0,8},{8,16},{16,24},{24,0},{1,9},{9,17},{17,25},{25,1},{2,10},{10... | collective-permute-start | bytes 147464 | tf_op jit(solution)/shard_map/ppermute | solution.py:84
  49.2 0.1 collective-permute-start.7
  49.3 1.8 %collective-permute-done.6 = f32[4,24,128]{2,0,1:T(4,128)S(1)} collective-permute-done((f32[4,24,128]{2,0,1:T(4,128)S(1)}, f32[4,24,128]{2,0,1:T(4,128)S(1)}, u32[]{:S(2)}, u32[]{:S(2)}) %collective-permute-start.6) | collective-permute-done | bytes 49184 | tf_op jit(solution)/shard_map/ppermute | solution.py:84
  51.1 2.7 %collective-permute-done.7 = f32[4,24,128]{2,0,1:T(4,128)S(1)} collective-permute-done((f32[4,24,128]{2,0,1:T(4,128)S(1)}, f32[4,24,128]{2,0,1:T(4,128)S(1)}, u32[]{:S(2)}, u32[]{:S(2)}) %collective-permute-start.7) | collective-permute-done | bytes 49184 | tf_op jit(solution)/shard_map/ppermute | solution.py:85
  53.8 0.1 concatenate.57
  53.9 0.1 collective-permute-start.9
  54.0 0.1 concatenate.56
  54.0 0.5 collective-permute-start.8
  54.6 1.0 collective-permute-done.9
  55.6 2.2 %collective-permute-done.8 = f32[4,12,128]{2,1,0:T(8,128)S(1)} collective-permute-done((f32[4,12,128]{2,1,0:T(8,128)S(1)}, f32[4,12,128]{2,1,0:T(8,128)S(1)}, u32[]{:S(2)}, u32[]{:S(2)}) %collective-permute-start.8) | collective-permute-done | bytes 24608 | tf_op jit(solution)/shard_map/ppermute | solution.py:84
  57.8 0.1 concatenate.58
  57.9 8.7 %apply.1.two_ref = f32[128,128]{1,0:T(8,128)S(1)} custom-call(s32[778]{0:T(1024)} %pair_list.1.list_hbm.refs_0_, f32[480,128]{1,0:T(8,128)S(1)} %bitcast.169, f32[3,32,128]{2,1,0:T(8,128)} %copy-done.2, bf16[388,256,256]{2,1,0:T(8,128)(2,1)} %get-tuple-element.11.refs_3_), custom_call_target="tpu_custom_call" | custom-call | tf_op jit(solution)/shard_map/apply/pallas_call | solution.py:674
  66.6 0.0 copy-start.1
  66.7 2.5 %collective-permute-start.10 = (f32[4,16,128]{2,1,0:T(8,128)S(1)}, f32[4,16,128]{2,1,0:T(8,128)S(1)}, u32[]{:S(2)}, u32[]{:S(2)}) collective-permute-start(f32[4,16,128]{2,1,0:T(8,128)S(1)} %fusion.2), channel_id=1, source_target_pairs={{0,4},{4,0},{1,5},{5,1},{2,6},{6,2},{3,7},{7,3},{8,12},{12,8},{9,1... | collective-permute-start | bytes 98312 | tf_op jit(solution)/shard_map/ppermute | solution.py:79
  69.2 2.0 %collective-permute-done.10 = f32[4,16,128]{2,1,0:T(8,128)S(1)} collective-permute-done((f32[4,16,128]{2,1,0:T(8,128)S(1)}, f32[4,16,128]{2,1,0:T(8,128)S(1)}, u32[]{:S(2)}, u32[]{:S(2)}) %collective-permute-start.10) | collective-permute-done | bytes 32800 | tf_op jit(solution)/shard_map/ppermute | solution.py:79
  71.3 3.1 %collective-permute-start.11 = (f32[4,24,128]{2,0,1:T(4,128)S(1)}, f32[4,24,128]{2,0,1:T(4,128)S(1)}, u32[]{:S(2)}, u32[]{:S(2)}) collective-permute-start(f32[4,24,128]{2,0,1:T(4,128)S(1)} %pad_maximum_fusion.5), channel_id=1, source_target_pairs={{0,8},{8,16},{16,24},{24,0},{1,9},{9,17},{17,25},{25,1},{2,10},{10... | collective-permute-start | bytes 147464 | tf_op jit(solution)/shard_map/ppermute | solution.py:84
  74.4 0.8 collective-permute-start.12
  75.2 2.4 %collective-permute-done.11 = f32[4,24,128]{2,0,1:T(4,128)S(1)} collective-permute-done((f32[4,24,128]{2,0,1:T(4,128)S(1)}, f32[4,24,128]{2,0,1:T(4,128)S(1)}, u32[]{:S(2)}, u32[]{:S(2)}) %collective-permute-start.11) | collective-permute-done | bytes 49184 | tf_op jit(solution)/shard_map/ppermute | solution.py:84
  77.6 0.9 collective-permute-done.12
  78.6 0.1 concatenate.62
  78.7 0.1 collective-permute-start.14
  78.7 0.1 concatenate.61
  78.8 0.5 collective-permute-start.13
  79.3 1.0 collective-permute-done.14
  80.3 2.2 %collective-permute-done.13 = f32[4,12,128]{2,1,0:T(8,128)S(1)} collective-permute-done((f32[4,12,128]{2,1,0:T(8,128)S(1)}, f32[4,12,128]{2,1,0:T(8,128)S(1)}, u32[]{:S(2)}, u32[]{:S(2)}) %collective-permute-start.13) | collective-permute-done | bytes 24608 | tf_op jit(solution)/shard_map/ppermute | solution.py:84
  82.5 0.1 concatenate.63
  82.6 0.0 copy-done
  82.6 8.9 %apply_last.1 = (f32[128,128]{1,0:T(8,128)S(1)}, f32[32,2,128]{2,1,0:T(2,128)S(1)}) custom-call(s32[778]{0:T(1024)} %pair_list.1.list_hbm.refs_0_, f32[480,128]{1,0:T(8,128)S(1)} %bitcast.168, f32[3,32,128]{2,1,0:T(8,128)} %copy-done.2, bf16[388,256,256]{2,1,0:T(8,128)(2,1)} %get-tuple-element.11.refs_3_, f32[128,128]{1,0:T(8,128)} %bitcast.174, ...), custom_call_target="tpu_custom_call" | custom-call | tf_op jit(solution)/shard_map/apply_last/pallas_call | solution.py:674
  91.5 0.0 copy-start.3
  91.5 11.9 %all_to_all.5.moments_ref = f32[32,2,128]{2,1,0:T(2,128)} all-to-all(f32[32,2,128]{2,1,0:T(2,128)S(1)} %get-tuple-element.12), channel_id=1, replica_groups=mesh['gx'=4,'gy'=2,'gz'=4] {'gx','gy','gz'}, dimensions={0} | all-to-all | bytes 65536 | tf_op jit(solution)/shard_map/all_to_all | solution.py:696
  103.4 0.0 copy-done.1
  103.4 0.0 copy-done.3
  103.4 1.8 %combine.1 = (f32[128,128]{1,0:T(8,128)}, f32[128,128]{1,0:T(8,128)}) custom-call(f32[32,2,128]{2,1,0:T(2,128)} %all_to_all.5.moments_ref, f32[128,128]{1,0:T(8,128)} %bitcast.175, f32[128,128]{1,0:T(8,128)} %copy-done, f32[128,128]{1,0:T(8,128)} %copy-done.1, f32[128,128]{1,0:T(8,128)} %copy-done.3), custom_call_target="tpu_custom_call" | custom-call | tf_op jit(solution)/shard_map/combine/pallas_call | solution.py:697
  (66 shorter events, 0.5 us)
Async XLA Ops:
  1.5 5.4 %collective-permute-start = (f32[9,16,128]{2,1,0:T(8,128)S(1)}, f32[9,16,128]{2,1,0:T(8,128)S(1)}, u32[]{:S(2)}, u32[]{:S(2)}) collective-permute-start(f32[9,16,128]{2,1,0:T(8,128)S(1)} %fusion.1), channel_id=1, source_target_pairs={{0,4},{4,0},{1,5},{5,1},{2,6},{6,2},{3,7},{7,3},{8,12},{12,8},{9,1... | collective-permute-start | bytes 221192 | tf_op jit(solution)/shard_map/ppermute | solution.py:79
  7.0 7.7 %collective-permute-start.1 = (f32[9,24,128]{2,1,0:T(8,128)S(1)}, f32[9,24,128]{2,1,0:T(8,128)S(1)}, u32[]{:S(2)}, u32[]{:S(2)}) collective-permute-start(f32[9,24,128]{2,1,0:T(8,128)S(1)} %pad_maximum_fusion.1), channel_id=1, source_target_pairs={{0,8},{8,16},{16,24},{24,0},{1,9},{9,17},{17,25},{25,1},{2,10},{10... | collective-permute-start | bytes 331784 | tf_op jit(solution)/shard_map/ppermute | solution.py:84
  9.1 6.0 %collective-permute-start.2 = (f32[9,24,128]{2,1,0:T(8,128)S(1)}, f32[9,24,128]{2,1,0:T(8,128)S(1)}, u32[]{:S(2)}, u32[]{:S(2)}) collective-permute-start(f32[9,24,128]{2,1,0:T(8,128)S(1)} %pad_maximum_fusion.2), channel_id=1, source_target_pairs={{8,0},{16,8},{24,16},{0,24},{9,1},{17,9},{25,17},{1,25},{10,2},{18... | collective-permute-start | bytes 331784 | tf_op jit(solution)/shard_map/ppermute | solution.py:85
  15.2 4.7 %collective-permute-start.4 = (f32[9,12,128]{2,1,0:T(8,128)S(1)}, f32[9,12,128]{2,1,0:T(8,128)S(1)}, u32[]{:S(2)}, u32[]{:S(2)}) collective-permute-start(f32[9,12,128]{2,1,0:T(8,128)S(1)} %concatenate.52), channel_id=1, source_target_pairs={{1,0},{2,1},{3,2},{0,3},{5,4},{6,5},{7,6},{4,7},{9,8},{10,9},{11,1... | collective-permute-start | bytes 165896 | tf_op jit(solution)/shard_map/ppermute | solution.py:85
  15.4 4.6 %collective-permute-start.3 = (f32[9,12,128]{2,1,0:T(8,128)S(1)}, f32[9,12,128]{2,1,0:T(8,128)S(1)}, u32[]{:S(2)}, u32[]{:S(2)}) collective-permute-start(f32[9,12,128]{2,1,0:T(8,128)S(1)} %concatenate.51), channel_id=1, source_target_pairs={{0,1},{1,2},{2,3},{3,0},{4,5},{5,6},{6,7},{7,4},{8,9},{9,10},{10,1... | collective-permute-start | bytes 165896 | tf_op jit(solution)/shard_map/ppermute | solution.py:84
  39.0 0.6 copy-start.2
  39.6 43.0 %copy-start = (f32[128,128]{1,0:T(8,128)}, f32[128,128]{1,0:T(8,128)S(1)}, u32[]{:S(2)}) copy-start(f32[128,128]{1,0:T(8,128)S(1)} %get-tuple-element.9.refs_5_.one_ref) | copy-start | bytes 196612
  39.6 5.0 %collective-permute-start.5 = (f32[4,16,128]{2,1,0:T(8,128)S(1)}, f32[4,16,128]{2,1,0:T(8,128)S(1)}, u32[]{:S(2)}, u32[]{:S(2)}) collective-permute-start(f32[4,16,128]{2,1,0:T(8,128)S(1)} %fusion.3), channel_id=1, source_target_pairs={{0,4},{4,0},{1,5},{5,1},{2,6},{6,2},{3,7},{7,3},{8,12},{12,8},{9,1... | collective-permute-start | bytes 98312 | tf_op jit(solution)/shard_map/ppermute | solution.py:79
  44.6 6.5 %collective-permute-start.6 = (f32[4,24,128]{2,0,1:T(4,128)S(1)}, f32[4,24,128]{2,0,1:T(4,128)S(1)}, u32[]{:S(2)}, u32[]{:S(2)}) collective-permute-start(f32[4,24,128]{2,0,1:T(4,128)S(1)} %pad_maximum_fusion.3), channel_id=1, source_target_pairs={{0,8},{8,16},{16,24},{24,0},{1,9},{9,17},{17,25},{25,1},{2,10},{10... | collective-permute-start | bytes 147464 | tf_op jit(solution)/shard_map/ppermute | solution.py:84
  49.2 4.6 %collective-permute-start.7 = (f32[4,24,128]{2,0,1:T(4,128)S(1)}, f32[4,24,128]{2,0,1:T(4,128)S(1)}, u32[]{:S(2)}, u32[]{:S(2)}) collective-permute-start(f32[4,24,128]{2,0,1:T(4,128)S(1)} %pad_maximum_fusion.4), channel_id=1, source_target_pairs={{8,0},{16,8},{24,16},{0,24},{9,1},{17,9},{25,17},{1,25},{10,2},{18... | collective-permute-start | bytes 147464 | tf_op jit(solution)/shard_map/ppermute | solution.py:85
  53.9 1.7 %collective-permute-start.9 = (f32[4,12,128]{2,1,0:T(8,128)S(1)}, f32[4,12,128]{2,1,0:T(8,128)S(1)}, u32[]{:S(2)}, u32[]{:S(2)}) collective-permute-start(f32[4,12,128]{2,1,0:T(8,128)S(1)} %concatenate.57), channel_id=1, source_target_pairs={{1,0},{2,1},{3,2},{0,3},{5,4},{6,5},{7,6},{4,7},{9,8},{10,9},{11,1... | collective-permute-start | bytes 73736 | tf_op jit(solution)/shard_map/ppermute | solution.py:85
  54.0 3.8 %collective-permute-start.8 = (f32[4,12,128]{2,1,0:T(8,128)S(1)}, f32[4,12,128]{2,1,0:T(8,128)S(1)}, u32[]{:S(2)}, u32[]{:S(2)}) collective-permute-start(f32[4,12,128]{2,1,0:T(8,128)S(1)} %concatenate.56), channel_id=1, source_target_pairs={{0,1},{1,2},{2,3},{3,0},{4,5},{5,6},{6,7},{7,4},{8,9},{9,10},{10,1... | collective-permute-start | bytes 73736 | tf_op jit(solution)/shard_map/ppermute | solution.py:84
  66.6 36.8 %copy-start.1 = (f32[128,128]{1,0:T(8,128)}, f32[128,128]{1,0:T(8,128)S(1)}, u32[]{:S(2)}) copy-start(f32[128,128]{1,0:T(8,128)S(1)} %apply.1.two_ref) | copy-start | bytes 196612
  66.7 4.5 %collective-permute-start.10 = (f32[4,16,128]{2,1,0:T(8,128)S(1)}, f32[4,16,128]{2,1,0:T(8,128)S(1)}, u32[]{:S(2)}, u32[]{:S(2)}) collective-permute-start(f32[4,16,128]{2,1,0:T(8,128)S(1)} %fusion.2), channel_id=1, source_target_pairs={{0,4},{4,0},{1,5},{5,1},{2,6},{6,2},{3,7},{7,3},{8,12},{12,8},{9,1... | collective-permute-start | bytes 98312 | tf_op jit(solution)/shard_map/ppermute | solution.py:79
  71.3 6.3 %collective-permute-start.11 = (f32[4,24,128]{2,0,1:T(4,128)S(1)}, f32[4,24,128]{2,0,1:T(4,128)S(1)}, u32[]{:S(2)}, u32[]{:S(2)}) collective-permute-start(f32[4,24,128]{2,0,1:T(4,128)S(1)} %pad_maximum_fusion.5), channel_id=1, source_target_pairs={{0,8},{8,16},{16,24},{24,0},{1,9},{9,17},{17,25},{25,1},{2,10},{10... | collective-permute-start | bytes 147464 | tf_op jit(solution)/shard_map/ppermute | solution.py:84
  74.4 4.1 %collective-permute-start.12 = (f32[4,24,128]{2,0,1:T(4,128)S(1)}, f32[4,24,128]{2,0,1:T(4,128)S(1)}, u32[]{:S(2)}, u32[]{:S(2)}) collective-permute-start(f32[4,24,128]{2,0,1:T(4,128)S(1)} %pad_maximum_fusion.6), channel_id=1, source_target_pairs={{8,0},{16,8},{24,16},{0,24},{9,1},{17,9},{25,17},{1,25},{10,2},{18... | collective-permute-start | bytes 147464 | tf_op jit(solution)/shard_map/ppermute | solution.py:85
  78.7 1.7 %collective-permute-start.14 = (f32[4,12,128]{2,1,0:T(8,128)S(1)}, f32[4,12,128]{2,1,0:T(8,128)S(1)}, u32[]{:S(2)}, u32[]{:S(2)}) collective-permute-start(f32[4,12,128]{2,1,0:T(8,128)S(1)} %concatenate.62), channel_id=1, source_target_pairs={{1,0},{2,1},{3,2},{0,3},{5,4},{6,5},{7,6},{4,7},{9,8},{10,9},{11,1... | collective-permute-start | bytes 73736 | tf_op jit(solution)/shard_map/ppermute | solution.py:85
  78.8 3.7 %collective-permute-start.13 = (f32[4,12,128]{2,1,0:T(8,128)S(1)}, f32[4,12,128]{2,1,0:T(8,128)S(1)}, u32[]{:S(2)}, u32[]{:S(2)}) collective-permute-start(f32[4,12,128]{2,1,0:T(8,128)S(1)} %concatenate.61), channel_id=1, source_target_pairs={{0,1},{1,2},{2,3},{3,0},{4,5},{5,6},{6,7},{7,4},{8,9},{9,10},{10,1... | collective-permute-start | bytes 73736 | tf_op jit(solution)/shard_map/ppermute | solution.py:84
  91.5 11.9 %copy-start.3 = (f32[128,128]{1,0:T(8,128)}, f32[128,128]{1,0:T(8,128)S(1)}, u32[]{:S(2)}) copy-start(f32[128,128]{1,0:T(8,128)S(1)} %get-tuple-element.13.three_ref) | copy-start | bytes 196612
